TPU v7x, 8 devices: a whole 2x2x1 slice. The times are simulated.
8 devices in a mesh: dp: 2 (over z, y), tp: 4 (over x, core).
Axes of the slice: x: 2, y: 2, z: 1, core: 2. Of those that a mesh axis runs over, the one named last changes fastest.
Arguments:
- irreps: bfloat16 [4096, 49, 128], P('dp', None, 'tp')
- norm_gain: float32 [7, 128], P(None, 'tp')
- w_up: bfloat16 [7, 128, 256], P(None, None, 'tp')
- w_gate: bfloat16 [128, 256], P(None, 'tp')
- w_down: bfloat16 [7, 256, 128], P(None, 'tp')
- to_grid: float32 [49, 196], replicated
- from_grid: float32 [196, 48], replicated
- grad_out: bfloat16 [4096, 49, 128], P('dp', None, 'tp')
Outputs:
- output 1: bfloat16 [4096, 49, 128], P('dp', None, 'tp')
- output 2: bfloat16 [4096, 49, 128], P('dp', None, 'tp')
- output 3: bfloat16 [7, 128, 256], P(None, None, 'tp')
- output 4: bfloat16 [128, 256], P(None, 'tp')
- output 5: bfloat16 [7, 256, 128], P(None, 'tp')
All inputs are finite; a program needn't handle non-finite values.
Results may differ from a plain program's by a relative error of at most 0.0127252.
Values are sent between devices in bfloat16 or wider.
A program may use at most 1 GiB of HBM per device.

v0:
```python
import math
import jax
import jax.numpy as jnp
from jax import lax
from jax.sharding import PartitionSpec as P

NORM_EPS = 1e-5


def expand_rows(per_degree):
    return jnp.concatenate([jnp.broadcast_to(per_degree[degree:degree + 1], (2 * degree + 1,) + per_degree.shape[1:]) for degree in range(per_degree.shape[0])], axis=0)


def degree_sums(per_coef):
    degrees = math.isqrt(per_coef.shape[0])
    return jnp.stack([per_coef[degree * degree:(degree + 1) * (degree + 1)].sum(axis=0) for degree in range(degrees)], axis=0)


def silu_grad(pre_act):
    sig_val = jax.nn.sigmoid(pre_act)
    return sig_val * (1.0 + pre_act * (1.0 - sig_val))


def hidden_block(xn_blk, grad_blk, up_rows, gate_loc, down_rows, grid_in, grid_back):
    hidden_act = jnp.einsum('nkc,kch->nkh', xn_blk, up_rows, preferred_element_type=jnp.float32).astype(jnp.bfloat16)
    pre_gate = jnp.dot(xn_blk[:, 0, :], gate_loc, preferred_element_type=jnp.float32).astype(jnp.bfloat16)
    gate_pre_f = pre_gate.astype(jnp.float32)
    gate_val = jax.nn.silu(gate_pre_f).astype(jnp.bfloat16)
    pre_grid = jnp.einsum('nkh,kg->ngh', hidden_act, grid_in, preferred_element_type=jnp.float32).astype(jnp.bfloat16)
    grid_pre_f = pre_grid.astype(jnp.float32)
    grid_val = jax.nn.silu(grid_pre_f).astype(jnp.bfloat16)
    back_proj = jnp.einsum('ngh,gk->nkh', grid_val, grid_back, preferred_element_type=jnp.float32).astype(jnp.bfloat16)
    mixed_act = jnp.concatenate([gate_val[:, None, :], back_proj], axis=1)
    part_out = jnp.einsum('nkh,khc->nkc', mixed_act, down_rows, preferred_element_type=jnp.float32).astype(jnp.bfloat16)
    d_mixed = jnp.einsum('nkc,khc->nkh', grad_blk, down_rows, preferred_element_type=jnp.float32).astype(jnp.bfloat16)
    g_down = jnp.einsum('nkh,nkc->khc', mixed_act, grad_blk, preferred_element_type=jnp.float32)
    d_grid = jnp.einsum('nkh,gk->ngh', d_mixed[:, 1:, :], grid_back, preferred_element_type=jnp.float32).astype(jnp.bfloat16)
    d_pre_grid = (d_grid.astype(jnp.float32) * silu_grad(grid_pre_f)).astype(jnp.bfloat16)
    d_hidden = jnp.einsum('ngh,kg->nkh', d_pre_grid, grid_in, preferred_element_type=jnp.float32).astype(jnp.bfloat16)
    d_pre_gate = (d_mixed[:, 0, :].astype(jnp.float32) * silu_grad(gate_pre_f)).astype(jnp.bfloat16)
    g_up = jnp.einsum('nkc,nkh->kch', xn_blk, d_hidden, preferred_element_type=jnp.float32)
    g_gate = jnp.einsum('nc,nh->ch', xn_blk[:, 0, :], d_pre_gate, preferred_element_type=jnp.float32)
    d_xn = jnp.einsum('nkh,kch->nkc', d_hidden, up_rows, preferred_element_type=jnp.float32)
    d_xn_zero = d_xn[:, 0, :] + jnp.einsum('nh,ch->nc', d_pre_gate, gate_loc, preferred_element_type=jnp.float32)
    d_xn = jnp.concatenate([d_xn_zero[:, None, :], d_xn[:, 1:, :]], axis=1).astype(jnp.bfloat16)
    return part_out, d_xn, g_up, g_gate, g_down


def hidden_pass(xn_full, grad_full, up_loc, gate_loc, down_loc, to_grid, from_grid):
    node_count, coef_count, channels = xn_full.shape
    blk_rows = math.gcd(node_count, 128)
    blk_count = node_count // blk_rows
    up_rows = expand_rows(up_loc)
    down_rows = expand_rows(down_loc)
    grid_in = to_grid.astype(jnp.bfloat16)
    grid_back = from_grid.astype(jnp.bfloat16)

    def scan_step(grad_sums, blk_pair):
        part_out, d_xn, g_up, g_gate, g_down = hidden_block(blk_pair[0], blk_pair[1], up_rows, gate_loc, down_rows, grid_in, grid_back)
        return (grad_sums[0] + g_up, grad_sums[1] + g_gate, grad_sums[2] + g_down), (part_out, d_xn)

    init_sums = (jnp.zeros(up_rows.shape, jnp.float32), jnp.zeros(gate_loc.shape, jnp.float32), jnp.zeros(down_rows.shape, jnp.float32))
    blk_shape = (blk_count, blk_rows, coef_count, channels)
    total_sums, (part_outs, d_xns) = lax.scan(scan_step, init_sums, (xn_full.reshape(blk_shape), grad_full.reshape(blk_shape)))
    full_shape = (node_count, coef_count, channels)
    return part_outs.reshape(full_shape), d_xns.reshape(full_shape), degree_sums(total_sums[0]), total_sums[1], degree_sums(total_sums[2])


def solution(mesh):
    tp_size = mesh.shape['tp']
    act_spec = P('dp', None, 'tp')
    in_specs = (act_spec, P(None, 'tp'), P(None, None, 'tp'), P(None, 'tp'), P(None, 'tp', None), P(None, None), P(None, None), act_spec)
    out_specs = (act_spec, act_spec, P(None, None, 'tp'), P(None, 'tp'), P(None, 'tp', None))

    def local_step(x_loc, gain_loc, up_loc, gate_loc, down_loc, to_grid, from_grid, grad_loc):
        coef_count = x_loc.shape[1]
        channels = x_loc.shape[2] * tp_size
        vec_count = channels * (coef_count - 1)
        x_f = x_loc.astype(jnp.float32)
        scalar = x_f[:, 0, :]
        vector = x_f[:, 1:, :]
        node_stats = jnp.stack([jnp.sum(scalar, axis=-1), jnp.sum(scalar * scalar, axis=-1), jnp.sum(vector * vector, axis=(1, 2))], axis=-1)
        node_stats = lax.psum(node_stats, 'tp')
        mean_s = node_stats[:, 0:1] / channels
        inv_s = lax.rsqrt(node_stats[:, 1:2] / channels - mean_s * mean_s + NORM_EPS)
        inv_v = lax.rsqrt(node_stats[:, 2] / vec_count + NORM_EPS)[:, None, None]
        hat_s = (scalar - mean_s) * inv_s
        hat_v = vector * inv_v
        gain_rows = expand_rows(gain_loc)
        xn_loc = jnp.concatenate([(hat_s * gain_rows[0])[:, None, :], hat_v * gain_rows[1:]], axis=1).astype(jnp.bfloat16)
        xn_full = lax.all_gather(xn_loc, 'tp', axis=2, tiled=True)
        grad_full = lax.all_gather(grad_loc, 'tp', axis=2, tiled=True)
        part_out, d_xn_part, g_up, g_gate, g_down = hidden_pass(xn_full, grad_full, up_loc, gate_loc, down_loc, to_grid, from_grid)
        ffn_delta = lax.psum_scatter(part_out, 'tp', scatter_dimension=2, tiled=True)
        out_loc = (x_f + ffn_delta.astype(jnp.float32)).astype(jnp.bfloat16)
        d_norm = lax.psum_scatter(d_xn_part, 'tp', scatter_dimension=2, tiled=True).astype(jnp.float32)
        d_hat_s = d_norm[:, 0, :] * gain_rows[0]
        d_hat_v = d_norm[:, 1:, :] * gain_rows[1:]
        back_stats = jnp.stack([jnp.sum(d_hat_s, axis=-1), jnp.sum(d_hat_s * hat_s, axis=-1), jnp.sum(d_hat_v * vector, axis=(1, 2))], axis=-1)
        back_stats = lax.psum(back_stats, 'tp')
        dx_s = inv_s * (d_hat_s - back_stats[:, 0:1] / channels - hat_s * back_stats[:, 1:2] / channels)
        dx_v = inv_v * d_hat_v - vector * (inv_v ** 3) * (back_stats[:, 2] / vec_count)[:, None, None]
        d_irreps = (jnp.concatenate([dx_s[:, None, :], dx_v], axis=1) + grad_loc.astype(jnp.float32)).astype(jnp.bfloat16)
        d_up = lax.psum(g_up, 'dp').astype(jnp.bfloat16)
        d_gate = lax.psum(g_gate, 'dp').astype(jnp.bfloat16)
        d_down = lax.psum(g_down, 'dp').astype(jnp.bfloat16)
        return out_loc, d_irreps, d_up, d_gate, d_down

    return jax.shard_map(local_step, mesh=mesh, in_specs=in_specs, out_specs=out_specs, check_vma=False)
```

profile of v0, /device:TPU:0, one launch (start us, length us, event | category | flops | bytes accessed | tf_op | source)
XLA Modules:
  0.0 1337.6 jit_solution(10705527437898268001)
XLA Ops:
  16.2 13.3 psum.35
  45.7 150.1 %all-gather.3.cloned.1.call-done = bf16[2048,49,128]{0,2,1:T(8,128)(2,1)} async-done(((bf16[2048,49,32]{0,2,1:T(8,128)(2,1)}), bf16[2048,49,128]{0,2,1:T(8,128)(2,1)}) %all-gather.3.cloned.1.call-update) | async-done | bytes 25690128 | tf_op jit(solution)/shard_map/all_gather | solution.py:91
  195.8 23.8 %copy.44 = bf16[784,8,16,128]{3,2,1,0:T(8,128)(2,1)} copy(bf16[784,8,16,128]{3,1,2,0:T(8,128)(2,1)} %bitcast.282) | data formatting | bytes 51380224
  219.6 33.1 %copy.39 = bf16[16,128,49,128]{3,1,2,0:T(8,128)(2,1)} copy(bf16[16,128,49,128]{1,0,3,2:T(8,128)(2,1)} %bitcast.280) | data formatting | bytes 51380224
  252.7 100.4 %all-gather.5.cloned.1.call-done = bf16[2048,49,128]{0,2,1:T(8,128)(2,1)} async-done(((bf16[2048,49,32]{0,2,1:T(8,128)(2,1)}), bf16[2048,49,128]{0,2,1:T(8,128)(2,1)}) %all-gather.5.cloned.1.call-update) | async-done | bytes 25690128 | tf_op jit(solution)/shard_map/all_gather | solution.py:92
  353.1 34.3 %copy.38 = bf16[2048,49,128]{2,0,1:T(8,128)(2,1)} copy(bf16[2048,49,128]{0,2,1:T(8,128)(2,1)} %all-gather.5.cloned.1.call-done) | data formatting | bytes 51380224 | tf_op jit(solution)/shard_map/all_gather | solution.py:92
  387.4 514.2 %while.19 = (s32[]{:T(128)}, f32[49,128,64]{1,2,0:T(8,128)}, f32[128,64]{0,1:T(8,128)S(1)}, f32[49,64,128]{2,1,0:T(8,128)}, bf16[16,128,49,128]{3,1,2,0:T(8,128)...) while((s32[]{:T(128)}, f32[49,128,64]{1,2,0:T(8,128)}, ...), condition=%wide.region_5.6_spmd.clone, body=%wide.region_4.5_spmd.clone.sunk | while | flops 1285439488 | bytes 80704024 | solution.py:64
  396.8 6.6 fusion.140
  428.4 6.6 fusion.140
  460.6 6.6 fusion.140
  492.8 6.6 fusion.140
  524.9 6.6 fusion.140
  557.1 6.6 fusion.140
  589.3 6.6 fusion.140
  621.5 6.6 fusion.140
  685.8 6.6 fusion.140
  717.9 6.6 fusion.140
  750.1 6.6 fusion.140
  782.2 6.6 fusion.140
  814.5 6.6 fusion.140
  846.7 6.6 fusion.140
  901.6 33.2 %copy.42 = bf16[16,128,49,128]{1,0,3,2:T(8,128)(2,1)} copy(bf16[16,128,49,128]{3,1,2,0:T(8,128)(2,1)} %get-tuple-element.77) | data formatting | bytes 51380224 | tf_op jit(solution)/shard_map/while | solution.py:64
  934.8 38.1 %reshape.144 = bf16[2048,49,128]{0,2,1:T(8,128)(2,1)} reshape(bf16[16,128,49,128]{1,0,3,2:T(8,128)(2,1)} %copy.42) | data formatting | bytes 51380224 | tf_op jit(solution)/shard_map/reshape | solution.py:66
  973.0 33.2 %copy.41 = bf16[16,128,49,128]{1,0,3,2:T(8,128)(2,1)} copy(bf16[16,128,49,128]{3,1,2,0:T(8,128)(2,1)} %get-tuple-element.76) | data formatting | bytes 51380224 | tf_op jit(solution)/shard_map/while | solution.py:64
  1006.2 38.2 %reshape.143 = bf16[2048,49,128]{0,2,1:T(8,128)(2,1)} reshape(bf16[16,128,49,128]{1,0,3,2:T(8,128)(2,1)} %copy.41) | data formatting | bytes 51380224 | tf_op jit(solution)/shard_map/reshape | solution.py:66
  1046.5 17.8 %all-reduce.2 = (bf16[7,128,64]{1,2,0:T(8,128)(2,1)}, bf16[128,64]{0,1:T(8,128)(2,1)}, bf16[7,64,128]{2,1,0:T(8,128)(2,1)}) all-reduce(f32[7,128,64]{1,2,0:T(8,128)S(1)} %constant_dynamic-update-slice_fusion.8, f32[128,64]{0,1:T(8,128)S(1)} %get-tuple-element.79, ...), channel_id=1, replica_groups=mesh['dp'=2,'tp'=4] {'dp'}, use_global_device_ids=true, to_apply=%region_18.19 | all-reduce | flops 122880 | bytes 737280 | tf_op jit(solution)/shard_map/psum | solution.py:104
  1064.3 80.9 %reduce-scatter.5.cloned.1.call-done = bf16[2048,49,32]{0,2,1:T(8,128)(2,1)} async-done(((bf16[2048,49,128]{0,2,1:T(8,128)(2,1)}), bf16[2048,49,32]{0,2,1:T(8,128)(2,1)}) %reduce-scatter.5.cloned.1.call-update) | async-done | bytes 6422544 | tf_op jit(solution)/shard_map/reduce_scatter | solution.py:96
  1150.9 9.4 multiply_reduce_fusion
  1160.3 10.3 psum.36
  1171.8 9.7 multiply_subtract_fusion
  1185.9 133.9 %reduce-scatter.3.cloned.1.call-done = bf16[2048,49,32]{0,2,1:T(8,128)(2,1)} async-done(((bf16[2048,49,128]{0,2,1:T(8,128)(2,1)}), bf16[2048,49,32]{0,2,1:T(8,128)(2,1)}) %reduce-scatter.3.cloned.1.call-update) | async-done | bytes 6422544 | tf_op jit(solution)/shard_map/reduce_scatter | solution.py:94
  1319.8 11.2 add_convert_fusion
  (542 shorter events, 458.0 us)
Async XLA Ops:
  7.2 188.6 %all-gather.3.cloned.1.call-start = ((), (), s32[]{:S(2)}) async-start(), calls=%async_computation.2 | async-start | bytes 32112640 | tf_op jit(solution)/shard_map/all_gather | solution.py:91
  16.2 19.2 %copy-start.21 = (f32[32]{0:T(128)}, f32[32]{0:T(128)S(1)}, u32[]{:S(2)}) copy-start(f32[32]{0:T(128)S(1)} %get-tuple-element.213) | copy-start | bytes 388
  29.6 5.8 copy-start.11
  29.6 5.8 copy-start.13
  29.6 5.8 copy-start.15
  39.8 313.3 %all-gather.5.cloned.1.call-start = ((), (), s32[]{:S(2)}) async-start(), calls=%async_computation.3 | async-start | bytes 32112640 | tf_op jit(solution)/shard_map/all_gather | solution.py:92
  40.6 1104.7 %reduce-scatter.5.cloned.1.call-start = ((), (), s32[]{:S(2)}) async-start(), calls=%async_computation.5 | async-start | bytes 32112640 | tf_op jit(solution)/shard_map/reduce_scatter | solution.py:96
  252.7 134.8 %copy-start.8 = (bf16[128,64]{0,1:T(8,128)(2,1)S(1)}, bf16[128,64]{0,1:T(8,128)(2,1)}, u32[]{:S(2)}) copy-start(bf16[128,64]{0,1:T(8,128)(2,1)} %param.13) | copy-start | bytes 49156
  395.8 9.7 copy-start.3
  427.4 9.7 copy-start.3
  459.6 9.7 copy-start.3
  491.8 9.7 copy-start.3
  523.9 9.7 copy-start.3
  556.1 9.7 copy-start.3
  588.3 9.7 copy-start.3
  620.5 9.7 copy-start.3
  652.7 9.7 copy-start.3
  684.8 9.7 copy-start.3
  716.9 9.7 copy-start.3
  749.1 9.7 copy-start.3
  781.2 9.7 copy-start.3
  813.5 9.7 copy-start.3
  845.7 9.7 copy-start.3
  877.8 9.7 copy-start.3
  972.9 346.9 %reduce-scatter.3.cloned.1.call-start = ((), (), s32[]{:S(2)}) async-start(), calls=%async_computation.4 | async-start | bytes 32112640 | tf_op jit(solution)/shard_map/reduce_scatter | solution.py:94
  1064.3 85.2 %copy-start.14 = (f32[2048,1]{0,1:T(1,128)S(1)}, f32[2048,1]{0,1:T(1,128)}, u32[]{:S(2)}) copy-start(f32[2048,1]{0,1:T(1,128)} %copy-done.13) | copy-start | bytes 24580
  1064.3 85.2 %copy-start.16 = (f32[2048,1]{0,1:T(1,128)S(1)}, f32[2048,1]{0,1:T(1,128)}, u32[]{:S(2)}) copy-start(f32[2048,1]{0,1:T(1,128)} %copy-done.15) | copy-start | bytes 24580
  1064.3 85.2 %copy-start.22 = (f32[32]{0:T(128)S(1)}, f32[32]{0:T(128)}, u32[]{:S(2)}) copy-start(f32[32]{0:T(128)} %copy-done.21) | copy-start | bytes 388
  1064.3 86.5 %copy-start.10 = (f32[48,32]{1,0:T(8,128)S(1)}, f32[48,32]{1,0:T(8,128)}, u32[]{:S(2)}) copy-start(f32[48,32]{1,0:T(8,128)} %copy-done.9) | copy-start | bytes 18436
  1149.6 10.7 copy-start.1
  1150.9 30.6 %slice-start = ((s8[6422528]{0:T(1024)(128)(4,1)}), s8[2228224]{0:T(1024)(128)(4,1)S(1)}, s32[]{:S(2)}) async-start(s8[6422528]{0:T(1024)(128)(4,1)} %bitcast.283), calls=%async_computation.6 | async-start | bytes 4456448
  1171.8 9.8 slice-start.1
  (58 other events, 163.9 us)
Sparse Core Ops, SparseCore 0:
  39.9 155.7 all-gather.2
  197.3 155.7 all-gather.4
  973.0 172.1 reduce-scatter.4
  1147.7 172.1 reduce-scatter.2
where the time goes:
time: 1350 us; the launch traced here: 1340 us
  waiting for transfers between devices  466 us (35%)
  matrix products  437 us (32%)
  local copies, waits for them, and re-layouts  294 us (22%)
  other arithmetic  83.6 us (6%)
  blocking collectives  41.4 us (3%)
  between operations  14.4 us (1%)
    all_gather x1, waiting for transfers between devices, local_step(): xn_full = lax.all_gather(xn_loc, 'tp', axis=2, tiled=True)  150 us
    reduce_scatter x1, waiting for transfers between devices, local_step(): lax.psum_scatter(part_out, 'tp', scatter_dimension=2, tiled=True)  134 us
    dot_general x16, matrix products, hidden_block(): jnp.einsum('ngh,kg->nkh', d_pre_grid, grid_in, preferred_element_type=jnp...  106 us
    all_gather x1, waiting for transfers between devices, local_step(): grad_full = lax.all_gather(grad_loc, 'tp', axis=2, tiled=True)  100 us
    reduce_scatter x1, waiting for transfers between devices, local_step(): lax.psum_scatter(d_xn_part, 'tp', scatter_dimension=2, tiled=True)  80.9 us
    while x2, local copies, waits for them, and re-layouts, hidden_pass(): lax.scan(scan_step, init_sums, (xn_full.reshape(blk_shape), grad_full.res...  66.4 us
    unnamed x68, local copies, waits for them, and re-layouts  65.8 us
    dot_general x16, matrix products, hidden_block(): jnp.einsum('nkh,nkc->khc', mixed_act, grad_blk, preferred_element_type=jn...  60.2 us
  transfers between devices with their start and end apart: 4, of which 4 were waited for; matrix products, arithmetic and copies ran while one was open for 12% of the time, Pallas kernels for 0%

commit v1 on v0

v1 whole, which is shorter than its diff:
```python
import jax
import jax.numpy as jnp
from jax import lax
from jax.experimental import pallas as pl
from jax.experimental.pallas import tpu as pltpu
from jax.sharding import PartitionSpec as P

NORM_EPS = 1e-5
F32 = jnp.float32
BF16 = jnp.bfloat16
MESH = pl.DeviceIdType.MESH
LANES = 128
STEP = 56


def degree_of(coef):
    total = (coef >= 1).astype(jnp.int32)
    for deg in range(2, 7):
        total = total + (coef >= deg * deg).astype(jnp.int32)
    return total


def mm(lhs, rhs):
    return jnp.dot(lhs, rhs, preferred_element_type=F32)


def mm_nt(lhs, rhs):
    return lax.dot_general(lhs, rhs, (((1,), (1,)), ((), ())), preferred_element_type=F32)


def sigmoid(val):
    return 0.5 * jnp.tanh(0.5 * val) + 0.5


def fused_kernel(x_hbm, g_hbm, up_hbm, gate_hbm, down_hbm, gain_hbm, tt_ref, t_ref, f_ref, ft_ref,
                 out_hbm, dx_hbm, gup_ref, ggate_ref, gdown_ref,
                 x_buf, g_buf, o_buf, n_buf, dn_buf, y0, y1, z0, z1,
                 wu, wg, wd, gain_in, wut, wgt, wdt, gain_b,
                 w_send, w_recv, w_loc, in_send, in_recv, in_loc, o_send, o_recv, o_loc):
    chunks, coefs = x_buf.shape[0], x_buf.shape[1]
    share = x_hbm.shape[1]
    own = chunks * LANES
    me = lax.axis_index('tp')
    mate = me ^ 1

    def rows(who, size):
        return pl.ds(pl.multiple_of(who * size, size), size)

    def lanes(who, chunk):
        return pl.ds(pl.multiple_of(who * own + chunk * LANES, LANES), LANES)

    barrier = pltpu.get_barrier_semaphore()
    for flip in (1, 2, 3):
        pl.semaphore_signal(barrier, inc=1, device_id={'tp': me ^ flip}, device_id_type=MESH)
    pl.semaphore_wait(barrier, 3)

    def weight_parts(who):
        hid = up_hbm.shape[1]
        return (wu.at[:, rows(who, hid), :], wd.at[:, rows(who, hid), :], wg.at[rows(who, hid), :], gain_in.at[who])

    sources = (up_hbm, down_hbm, gate_hbm, gain_hbm)

    def weight_copies(flip):
        if flip == 3:
            parts = weight_parts(me ^ 2)
            pairs = zip(parts, parts)
            peer = mate
        else:
            pairs = zip(sources, weight_parts(me))
            peer = me ^ flip
        return [pltpu.make_async_remote_copy(src, dst, w_send.at[flip, i], w_recv.at[flip, i], device_id={'tp': peer}, device_id_type=MESH)
                for i, (src, dst) in enumerate(pairs)]

    own_weights = [pltpu.make_async_copy(src, dst, w_loc.at[i]) for i, (src, dst) in enumerate(zip(sources, weight_parts(me)))]
    far_weights, mate_weights, relay_weights = weight_copies(2), weight_copies(1), weight_copies(3)
    for copy in far_weights + mate_weights + own_weights:
        copy.start()

    def input_copy(tensor, chunk, flip):
        src, buf = ((x_hbm, x_buf), (g_hbm, g_buf))[tensor]
        return pltpu.make_async_remote_copy(
            src.at[:, :, lanes(me ^ flip, chunk)], buf.at[chunk, :, rows(me, share), :],
            in_send.at[tensor, chunk, flip], in_recv.at[tensor, chunk, flip],
            device_id={'tp': me ^ flip}, device_id_type=MESH)

    def input_local(tensor, chunk):
        src, buf = ((x_hbm, x_buf), (g_hbm, g_buf))[tensor]
        return pltpu.make_async_copy(src.at[:, :, lanes(me, chunk)], buf.at[chunk, :, rows(me, share), :], in_loc.at[tensor, chunk])

    def output_copy(tensor, chunk, flip):
        buf, dst = ((o_buf, out_hbm), (g_buf, dx_hbm))[tensor]
        return pltpu.make_async_remote_copy(
            buf.at[chunk, :, rows(me ^ flip, share), :], dst.at[:, :, lanes(me, chunk)],
            o_send.at[tensor, chunk, flip], o_recv.at[tensor, chunk, flip],
            device_id={'tp': me ^ flip}, device_id_type=MESH)

    def output_local(tensor, chunk):
        buf, dst = ((o_buf, out_hbm), (g_buf, dx_hbm))[tensor]
        return pltpu.make_async_copy(buf.at[chunk, :, rows(me, share), :], dst.at[:, :, lanes(me, chunk)], o_loc.at[tensor, chunk])

    def start_inputs(chunk, carry):
        for flip in (2, 3, 1):
            for tensor in (0, 1):
                input_copy(tensor, chunk, flip).start()
        for tensor in (0, 1):
            input_local(tensor, chunk).start()
        return carry

    lax.fori_loop(0, chunks, start_inputs, 0)

    gup_ref[...] = jnp.zeros_like(gup_ref)
    ggate_ref[...] = jnp.zeros_like(ggate_ref)
    gdown_ref[...] = jnp.zeros_like(gdown_ref)
    blank = jnp.zeros((LANES, LANES), F32)
    for pad in range(coefs, STEP):
        for ref in (y0, y1, z0, z1):
            ref[pl.ds(pad, LANES, stride=STEP), :] = blank
    for ref in (z0, z1):
        ref[pl.ds(0, LANES, stride=STEP), :] = blank

    for far, relay in zip(far_weights, relay_weights):
        far.wait_recv()
        relay.start()
    for copy in far_weights:
        copy.wait_send()
    for copy in mate_weights + relay_weights + own_weights:
        copy.wait()

    def turn(deg, carry):
        wut[deg] = wu[deg].astype(F32).T.astype(BF16)
        wdt[deg] = wd[deg].astype(F32).T.astype(BF16)
        return carry

    degrees = wu.shape[0]
    lax.fori_loop(0, degrees, turn, 0)
    wgt[...] = wg[...].astype(F32).T.astype(BF16)
    gains = jnp.concatenate([gain_in[i][:, :share] for i in range(gain_in.shape[0])], axis=1)
    gains = jnp.concatenate([gains] * (LANES // gains.shape[0]), axis=0).T
    for deg in range(degrees):
        gain_b[deg] = jnp.broadcast_to(gains[:, deg:deg + 1], (LANES, LANES))

    inv_chan = 1.0 / LANES
    inv_vec = 1.0 / (LANES * (coefs - 1))

    def chunk_step(chunk, carry):
        for flip in (2, 3, 1):
            for tensor in (0, 1):
                input_copy(tensor, chunk, flip).wait_recv()
        for tensor in (0, 1):
            input_local(tensor, chunk).wait()

        def square_sum(k, acc):
            val = x_buf[chunk, k].astype(F32)
            return acc + val * val

        sq = lax.fori_loop(1, coefs, square_sum, jnp.zeros((LANES, LANES), F32), unroll=8)
        inv_v = lax.rsqrt(jnp.sum(sq, axis=0, keepdims=True) * inv_vec + NORM_EPS)
        scalar = x_buf[chunk, 0].astype(F32)
        cent = scalar - jnp.sum(scalar, axis=0, keepdims=True) * inv_chan
        inv_s = lax.rsqrt(jnp.sum(cent * cent, axis=0, keepdims=True) * inv_chan + NORM_EPS)
        hat_s = cent * inv_s
        n_zero = (hat_s * gain_b[0]).astype(BF16)
        n_buf[0] = n_zero
        y_zero = mm(wu[0], n_zero)
        y0[pl.ds(0, LANES, stride=STEP), :] = y_zero[:LANES]
        y1[pl.ds(0, LANES, stride=STEP), :] = y_zero[LANES:]

        def up_step(k, carry):
            deg = degree_of(k)
            n_k = (x_buf[chunk, k].astype(F32) * inv_v * gain_b[deg]).astype(BF16)
            n_buf[k] = n_k
            y_k = mm(wu[deg], n_k)
            y0[pl.ds(k, LANES, stride=STEP), :] = y_k[:LANES]
            y1[pl.ds(k, LANES, stride=STEP), :] = y_k[LANES:]
            dm_k = mm(wd[deg], g_buf[chunk, k])
            z0[pl.ds(k, LANES, stride=STEP), :] = dm_k[:LANES]
            z1[pl.ds(k, LANES, stride=STEP), :] = dm_k[LANES:]
            return carry

        lax.fori_loop(1, coefs, up_step, 0, unroll=4)

        def grid_step(j, carry):
            span = pl.ds(pl.multiple_of(j * STEP, 8), STEP)
            y_j = jnp.concatenate([y0[span, :], y1[span, :]], axis=1).astype(BF16)
            dm_j = jnp.concatenate([z0[span, :], z1[span, :]], axis=1).astype(BF16)
            u = mm(tt_ref[...], y_j).astype(BF16).astype(F32)
            sig = sigmoid(u)
            act = u * sig
            z_j = mm(ft_ref[...], act.astype(BF16))
            z0[span, :] = z_j[:, :LANES]
            z1[span, :] = z_j[:, LANES:]
            ds = mm(f_ref[...], dm_j).astype(BF16).astype(F32)
            du = (ds * (sig + act * (1.0 - sig))).astype(BF16)
            dy_j = mm(t_ref[...], du)
            y0[span, :] = dy_j[:, :LANES]
            y1[span, :] = dy_j[:, LANES:]
            return carry

        lax.fori_loop(0, LANES, grid_step, 0, unroll=2)

        def hidden_grad(k):
            picked = pl.ds(k, LANES, stride=STEP)
            return jnp.concatenate([y0[picked, :], y1[picked, :]], axis=0).astype(BF16)

        g_zero = g_buf[chunk, 0]
        n_zero = n_buf[0]
        pre = mm(wg[...], n_zero).astype(BF16).astype(F32)
        sig = sigmoid(pre)
        gate = pre * sig
        dm_zero = mm(wd[0], g_zero).astype(BF16).astype(F32)
        d_pre = (dm_zero * (sig + gate * (1.0 - sig))).astype(BF16)
        gate = gate.astype(BF16)
        o_buf[chunk, 0] = (x_buf[chunk, 0].astype(F32) + mm(wdt[0], gate)).astype(BF16)
        gdown_ref[0] += mm_nt(gate, g_zero)
        dy_zero = hidden_grad(0)
        gup_ref[0] += mm_nt(dy_zero, n_zero)
        ggate_ref[...] += mm_nt(d_pre, n_zero)
        dn_zero = (mm(wut[0], dy_zero) + mm(wgt[...], d_pre)).astype(BF16).astype(F32)

        def down_step(k, acc):
            deg = degree_of(k)
            picked = pl.ds(k, LANES, stride=STEP)
            m_k = jnp.concatenate([z0[picked, :], z1[picked, :]], axis=0).astype(BF16)
            dy_k = hidden_grad(k)
            x_k = x_buf[chunk, k].astype(F32)
            o_buf[chunk, k] = (x_k + mm(wdt[deg], m_k)).astype(BF16)
            gdown_ref[deg] += mm_nt(m_k, g_buf[chunk, k])
            dn_k = mm(wut[deg], dy_k).astype(BF16)
            dn_buf[k] = dn_k
            gup_ref[deg] += mm_nt(dy_k, n_buf[k])
            return acc + dn_k.astype(F32) * gain_b[deg] * x_k

        dot_v = lax.fori_loop(1, coefs, down_step, jnp.zeros((LANES, LANES), F32), unroll=4)
        for flip in (2, 3, 1):
            output_copy(0, chunk, flip).start()
        output_local(0, chunk).start()

        z0[pl.ds(0, LANES, stride=STEP), :] = blank
        z1[pl.ds(0, LANES, stride=STEP), :] = blank
        dh_s = dn_zero * gain_b[0]
        mean_d = jnp.sum(dh_s, axis=0, keepdims=True) * inv_chan
        mean_dx = jnp.sum(dh_s * hat_s, axis=0, keepdims=True) * inv_chan
        dx_s = inv_s * (dh_s - mean_d - hat_s * mean_dx)
        g_buf[chunk, 0] = (dx_s + g_zero.astype(F32)).astype(BF16)
        coef_v = inv_v * inv_v * inv_v * (jnp.sum(dot_v, axis=0, keepdims=True) * inv_vec)

        def back_step(k, carry):
            dh = dn_buf[k].astype(F32) * gain_b[degree_of(k)]
            dx = inv_v * dh - x_buf[chunk, k].astype(F32) * coef_v
            g_buf[chunk, k] = (dx + g_buf[chunk, k].astype(F32)).astype(BF16)
            return carry

        lax.fori_loop(1, coefs, back_step, 0, unroll=4)
        for flip in (2, 3, 1):
            output_copy(1, chunk, flip).start()
        output_local(1, chunk).start()
        return carry

    lax.fori_loop(0, chunks, chunk_step, 0)

    def finish(chunk, carry):
        for tensor in (0, 1):
            for flip in (2, 3, 1):
                input_copy(tensor, chunk, flip).wait_send()
                output_copy(tensor, chunk, flip).wait()
            output_local(tensor, chunk).wait()
        return carry

    lax.fori_loop(0, chunks, finish, 0)


def solution(mesh):
    tp_size = mesh.shape['tp']
    act_spec = P('dp', None, 'tp')
    in_specs = (act_spec, P(None, 'tp'), P(None, None, 'tp'), P(None, 'tp'), P(None, 'tp', None), P(None, None), P(None, None), act_spec)
    out_specs = (act_spec, act_spec, P(None, None, 'tp'), P(None, 'tp'), P(None, 'tp', None))

    def local_step(x_loc, gain_loc, up_loc, gate_loc, down_loc, to_grid, from_grid, grad_loc):
        nodes, coefs, share = x_loc.shape
        degrees, channels, hid = up_loc.shape
        hidden = hid * tp_size
        points = to_grid.shape[1]
        pts = -(-points // 8) * 8
        chunks = nodes // tp_size // LANES
        x_t = jnp.transpose(x_loc, (1, 2, 0))
        g_t = jnp.transpose(grad_loc, (1, 2, 0))
        up_t = jnp.transpose(up_loc, (0, 2, 1))
        gate_t = jnp.transpose(gate_loc, (1, 0))
        gain_pad = jnp.pad(gain_loc, ((0, 8 - degrees), (0, LANES - share)))
        t_pad = jnp.pad(to_grid.astype(BF16), ((0, STEP - coefs), (0, pts - points)))
        f_pad = jnp.pad(from_grid.astype(BF16), ((0, pts - points), (1, STEP - coefs)))
        hbm = pl.BlockSpec(memory_space=pl.ANY)
        vmem = pl.BlockSpec(memory_space=pltpu.VMEM)
        dma = pltpu.SemaphoreType.DMA
        act = (chunks, coefs, channels, LANES)
        wide = pltpu.VMEM((LANES * STEP, LANES), F32)
        out_t, dx_t, g_up, g_gate, g_down = pl.pallas_call(
            fused_kernel,
            out_shape=(
                jax.ShapeDtypeStruct(x_t.shape, BF16),
                jax.ShapeDtypeStruct(x_t.shape, BF16),
                jax.ShapeDtypeStruct((degrees, hidden, channels), F32),
                jax.ShapeDtypeStruct((hidden, channels), F32),
                jax.ShapeDtypeStruct((degrees, hidden, channels), F32)),
            in_specs=[hbm] * 6 + [vmem] * 4,
            out_specs=(hbm, hbm, vmem, vmem, vmem),
            scratch_shapes=[
                pltpu.VMEM(act, BF16), pltpu.VMEM(act, BF16), pltpu.VMEM(act, BF16),
                pltpu.VMEM(act[1:], BF16), pltpu.VMEM(act[1:], BF16),
                wide, wide, wide, wide,
                pltpu.VMEM((degrees, hidden, channels), BF16), pltpu.VMEM((hidden, channels), BF16),
                pltpu.VMEM((degrees, hidden, channels), BF16), pltpu.VMEM((tp_size, 8, LANES), F32),
                pltpu.VMEM((degrees, channels, hidden), BF16), pltpu.VMEM((channels, hidden), BF16),
                pltpu.VMEM((degrees, channels, hidden), BF16), pltpu.VMEM((degrees, channels, LANES), F32),
                dma((4, 4)), dma((4, 4)), dma((4,)),
                dma((2, chunks, 4)), dma((2, chunks, 4)), dma((2, chunks)),
                dma((2, chunks, 4)), dma((2, chunks, 4)), dma((2, chunks))],
            compiler_params=pltpu.CompilerParams(collective_id=0, has_side_effects=True, vmem_limit_bytes=62 * 1024 * 1024),
            name='fused',
        )(x_t, g_t, up_t, gate_t, down_loc, gain_pad, t_pad.T, t_pad, f_pad, f_pad.T)
        back = lambda val: jnp.transpose(val, (2, 0, 1))

        def reduce(val, dim):
            return lax.psum(lax.psum_scatter(val, 'tp', scatter_dimension=dim, tiled=True), 'dp').astype(BF16)

        d_up = jnp.transpose(reduce(g_up, 1), (0, 2, 1))
        d_gate = jnp.transpose(reduce(g_gate, 0), (1, 0))
        return back(out_t), back(dx_t), d_up, d_gate, reduce(g_down, 1)

    return jax.shard_map(local_step, mesh=mesh, in_specs=in_specs, out_specs=out_specs, check_vma=False)
```

time: 1350 us -> 478 us (0.35)
  matrix products: 437 us -> 0 us
  waiting for transfers between devices: 466 us -> 56 us
  Pallas kernels: 0 us -> 375 us
  local copies, waits for them, and re-layouts: 294 us -> 13.7 us
  other arithmetic: 83.6 us -> 1.63 us
  blocking collectives: 41.4 us -> 17.3 us
    dot_general x192 -> x0, matrix products: 437 us -> none  [the longest x16 106 us: hidden_block(): jnp.einsum('ngh,kg->nkh', d_pre_grid, grid_in, preferred_element_type=jnp...]
    pallas_call x0 -> x1, Pallas kernels: none -> 375 us  [local_step(): pl.pallas_call(fused_kernel, out_shape=(jax.ShapeDtypeStruct(x_t.shape, B...]
    all_gather x2 -> x0, waiting for transfers between devices: 251 us -> none  [the longest x1 150 us: local_step(): xn_full = lax.all_gather(xn_loc, 'tp', axis=2, tiled=True)]
    reduce_scatter x2 -> x3, waiting for transfers between devices: 215 us -> 54.6 us  [reduce(): lax.psum_scatter(val, 'tp', scatter_dimension=dim, tiled=True)]
    reshape x2 -> x0, local copies, waits for them, and re-layouts: 76.3 us -> none  [the longest x1 38.2 us: hidden_pass(): part_outs.reshape(full_shape)]
    while x130 -> x0, local copies, waits for them, and re-layouts: 70.8 us -> none  [the longest x2 66.4 us: hidden_pass(): lax.scan(scan_step, init_sums, (xn_full.reshape(blk_shape), grad_full.res...]
    unnamed x68 -> x7, local copies, waits for them, and re-layouts: 65.8 us -> 9.74 us
    all_gather x1 -> x0, local copies, waits for them, and re-layouts: 34.3 us -> none  [local_step(): grad_full = lax.all_gather(grad_loc, 'tp', axis=2, tiled=True)]
  transfers between devices with their start and end apart: 4 -> 3, of which waited for: 4 -> 3; matrix products, arithmetic and copies ran while one was open for 12% -> 0% of each run, Pallas kernels for 0% -> 0%
where the time goes in v1:
time: 478 us; the launch traced here: 477 us
  Pallas kernels  375 us (78%)
  waiting for transfers between devices  56 us (12%)
  blocking collectives  17.3 us (4%)
  between operations  13.8 us (3%)
  local copies, waits for them, and re-layouts  13.7 us (3%)
    pallas_call x1, Pallas kernels, local_step(): pl.pallas_call(fused_kernel, out_shape=(jax.ShapeDtypeStruct(x_t.shape, B...  375 us
    reduce_scatter x3, waiting for transfers between devices, reduce(): lax.psum_scatter(val, 'tp', scatter_dimension=dim, tiled=True)  54.6 us
    psum x1, blocking collectives, reduce(): lax.psum(lax.psum_scatter(val, 'tp', scatter_dimension=dim, tiled=True),...  17.3 us
    unnamed x7, local copies, waits for them, and re-layouts  9.74 us
  transfers between devices with their start and end apart: 3, of which 3 were waited for; matrix products, arithmetic and copies ran while one was open for 0% of the time, Pallas kernels for 0%

profile of v1, /device:TPU:0, one launch (start us, length us, event | category | flops | bytes accessed | tf_op | source)
XLA Modules:
  0.0 477.2 jit_solution(17616582880877969491)
XLA Ops:
  7.2 0.0 reduce-scatter.6.cloned.1.call-start
  7.2 0.8 convert_element_type.22
  8.0 0.1 copy.15
  8.1 0.6 pad_bitcast_fusion.ft_ref
  8.8 0.8 convert_element_type.21
  9.6 0.6 fusion
  10.2 0.7 copy.13.tt_ref
  10.9 0.7 pad.14.clone.f_ref
  11.6 1.3 pad.12.gain_hbm
  12.9 374.7 %fused.1 = (bf16[49,32,2048]{2,1,0:T(8,128)(2,1)}, bf16[49,32,2048]{2,1,0:T(8,128)(2,1)}, f32[7,256,128]{2,1,0:T(8,128)}, f32[256,128]{1,0:T(8,128)}, f32[7,256,128]{2,1,0:T(8,128)}) custom-call(bf16[49,32,2048]{2,1,0:T(8,128)(2,1)} %bitcast.16, bf16[49,32,2048]{2,1,0:T(8,128)(2,1)} %bitcast.17, bf16[7,64,128]{2,1,0:T(8,128)(2,1)} %bitcast.22, ...), custom_call_target="tpu_custom_call" | custom-call | tf_op jit(solution)/shard_map/fused/pallas_call | solution.py:297
  387.6 0.0 reduce-scatter.6.cloned.1.call-update
  387.6 0.0 reduce-scatter.4.cloned.1.call-start
  387.7 0.7 reduce-scatter.4.cloned.1.call-update
  388.4 0.0 reduce-scatter.8.cloned.1.call-start
  388.4 0.7 reduce-scatter.8.cloned.1.call-update
  389.1 12.8 %reduce-scatter.6.cloned.1.call-done = f32[64,128]{1,0:T(8,128)} async-done(((f32[256,128]{1,0:T(8,128)}), f32[64,128]{1,0:T(8,128)}) %reduce-scatter.6.cloned.1.call-update) | async-done | bytes 32784 | tf_op jit(solution)/shard_map/reduce_scatter | solution.py:324
  402.0 20.9 %reduce-scatter.4.cloned.1.call-done = f32[7,64,128]{2,1,0:T(8,128)} async-done(((f32[7,256,128]{2,1,0:T(8,128)}), f32[7,64,128]{2,1,0:T(8,128)}) %reduce-scatter.4.cloned.1.call-update) | async-done | bytes 229392 | tf_op jit(solution)/shard_map/reduce_scatter | solution.py:324
  422.9 20.9 %reduce-scatter.8.cloned.1.call-done = f32[7,64,128]{2,1,0:T(8,128)} async-done(((f32[7,256,128]{2,1,0:T(8,128)}), f32[7,64,128]{2,1,0:T(8,128)}) %reduce-scatter.8.cloned.1.call-update) | async-done | bytes 229392 | tf_op jit(solution)/shard_map/reduce_scatter | solution.py:324
  443.8 0.0 slice-start
  443.8 17.3 %all-reduce.5 = (bf16[7,64,128]{2,1,0:T(8,128)(2,1)}, bf16[64,128]{1,0:T(8,128)(2,1)}, bf16[7,64,128]{2,1,0:T(8,128)(2,1)}) all-reduce(f32[7,64,128]{2,1,0:T(8,128)} %reduce-scatter.4.cloned.1.call-done, f32[64,128]{1,0:T(8,128)} %reduce-scatter.6.cloned.1.call-done, ...), channel_id=1, replica_groups=mesh['dp'=2,'tp'=4] {'dp'}, use_global_device_ids=true, to_apply=%region_1.2 | all-reduce | flops 122880 | bytes 737280 | tf_op jit(solution)/shard_map/psum | solution.py:324
  461.0 0.0 slice-start.1
  461.0 6.9 %copy.24 = bf16[2048,49,32]{0,2,1:T(8,128)(2,1)} copy(bf16[2048,49,32]{0,2,1:T(8,128)(2,1)} %bitcast.21) | data formatting | bytes 12845056
  467.9 0.0 slice-done
  467.9 0.0 slice-done.1
  467.9 2.7 copy.25
  (1 shorter events, 0.0 us)
Async XLA Ops:
  7.2 394.8 %reduce-scatter.6.cloned.1.call-start = ((), (), s32[]{:S(2)}) async-start(), calls=%async_computation.4 | async-start | bytes 163840 | tf_op jit(solution)/shard_map/reduce_scatter | solution.py:324
  387.6 35.2 %reduce-scatter.4.cloned.1.call-start = ((), (), s32[]{:S(2)}) async-start(), calls=%async_computation.3 | async-start | bytes 1146880 | tf_op jit(solution)/shard_map/reduce_scatter | solution.py:324
  388.4 55.4 %reduce-scatter.8.cloned.1.call-start = ((), (), s32[]{:S(2)}) async-start(), calls=%async_computation.5 | async-start | bytes 1146880 | tf_op jit(solution)/shard_map/reduce_scatter | solution.py:324
  443.8 24.2 %slice-start = ((s8[6422528]{0:T(1024)(128)(4,1)}), s8[2228224]{0:T(1024)(128)(4,1)S(1)}, s32[]{:S(2)}) async-start(s8[6422528]{0:T(1024)(128)(4,1)} %bitcast.18), calls=%async_computation.6 | async-start | bytes 4456448
  461.0 6.9 %slice-start.1 = ((s8[6422528]{0:T(1024)(128)(4,1)}), s8[4194304]{0:T(1024)(128)(4,1)S(1)}, s32[]{:S(2)}) async-start(s8[6422528]{0:T(1024)(128)(4,1)} %bitcast.18), calls=%async_computation.7 | async-start | bytes 8388608
Sparse Core Ops, SparseCore 0:
  387.8 14.1 reduce-scatter.5
  404.5 18.3 reduce-scatter.3
  425.4 18.3 reduce-scatter.7

commit v2 on v1

--- a/solution.py
+++ b/solution.py
@@ -11,6 +11,7 @@
 MESH = pl.DeviceIdType.MESH
 LANES = 128
 STEP = 56
+WIDE = 4
 
 
 def degree_of(coef):
@@ -32,16 +33,19 @@
     return 0.5 * jnp.tanh(0.5 * val) + 0.5
 
 
-def fused_kernel(x_hbm, g_hbm, up_hbm, gate_hbm, down_hbm, gain_hbm, tt_ref, t_ref, f_ref, ft_ref,
-                 out_hbm, dx_hbm, gup_ref, ggate_ref, gdown_ref,
+def fused_kernel(x_hbm, g_hbm, up_hbm, gate_hbm, down_hbm, gain_hbm, tg_ref, fg_ref,
+                 out_hbm, dx_hbm, dup_ref, dgate_ref, ddown_ref,
                  x_buf, g_buf, o_buf, n_buf, dn_buf, y0, y1, z0, z1,
                  wu, wg, wd, gain_in, wut, wgt, wdt, gain_b,
-                 w_send, w_recv, w_loc, in_send, in_recv, in_loc, o_send, o_recv, o_loc):
+                 tt_ref, t_ref, f_ref, ft_ref, pad_buf, u_buf, s_buf, act_buf, du_buf,
+                 g_sum, half_buf, mate_buf, far_buf, fin_buf,
+                 w_send, w_recv, w_loc, in_send, in_recv, in_loc, o_send, o_recv, o_loc, r_send, r_recv):
     chunks, coefs = x_buf.shape[0], x_buf.shape[1]
     share = x_hbm.shape[1]
     own = chunks * LANES
     me = lax.axis_index('tp')
     mate = me ^ 1
+    side = lax.axis_index('dp')
 
     def rows(who, size):
         return pl.ds(pl.multiple_of(who * size, size), size)
@@ -52,7 +56,8 @@
     barrier = pltpu.get_barrier_semaphore()
     for flip in (1, 2, 3):
         pl.semaphore_signal(barrier, inc=1, device_id={'tp': me ^ flip}, device_id_type=MESH)
-    pl.semaphore_wait(barrier, 3)
+    pl.semaphore_signal(barrier, inc=1, device_id={'dp': 1 - side}, device_id_type=MESH)
+    pl.semaphore_wait(barrier, 4)
 
     def weight_parts(who):
         hid = up_hbm.shape[1]
@@ -98,6 +103,15 @@
         buf, dst = ((o_buf, out_hbm), (g_buf, dx_hbm))[tensor]
         return pltpu.make_async_copy(buf.at[chunk, :, rows(me, share), :], dst.at[:, :, lanes(me, chunk)], o_loc.at[tensor, chunk])
 
+    def start_outputs(tensor, chunk):
+        @pl.when(chunk < chunks - 1)
+        def _():
+            for flip in (2, 3):
+                output_copy(tensor, chunk, flip).start()
+
+        output_copy(tensor, chunk, 1).start()
+        output_local(tensor, chunk).start()
+
     def start_inputs(chunk, carry):
         for flip in (2, 3, 1):
             for tensor in (0, 1):
@@ -108,15 +122,24 @@
 
     lax.fori_loop(0, chunks, start_inputs, 0)
 
-    gup_ref[...] = jnp.zeros_like(gup_ref)
-    ggate_ref[...] = jnp.zeros_like(ggate_ref)
-    gdown_ref[...] = jnp.zeros_like(gdown_ref)
+    g_sum[...] = jnp.zeros_like(g_sum)
     blank = jnp.zeros((LANES, LANES), F32)
     for pad in range(coefs, STEP):
         for ref in (y0, y1, z0, z1):
             ref[pl.ds(pad, LANES, stride=STEP), :] = blank
     for ref in (z0, z1):
         ref[pl.ds(0, LANES, stride=STEP), :] = blank
+
+    points = tg_ref.shape[1]
+    pts = t_ref.shape[1]
+    pad_buf[...] = jnp.zeros_like(pad_buf)
+    pad_buf[:coefs, :points] = tg_ref[...].astype(BF16).astype(F32)
+    t_ref[...] = pad_buf[:STEP, :pts].astype(BF16)
+    tt_ref[...] = (0.5 * pad_buf[...]).T[:pts, :STEP].astype(BF16)
+    pad_buf[...] = jnp.zeros_like(pad_buf)
+    pad_buf[1:coefs, :points] = fg_ref[...].astype(BF16).astype(F32)
+    ft_ref[...] = pad_buf[:STEP, :pts].astype(BF16)
+    f_ref[...] = (0.5 * pad_buf[...]).T[:pts, :STEP].astype(BF16)
 
     for far, relay in zip(far_weights, relay_weights):
         far.wait_recv()
@@ -134,8 +157,9 @@
     degrees = wu.shape[0]
     lax.fori_loop(0, degrees, turn, 0)
     wgt[...] = wg[...].astype(F32).T.astype(BF16)
-    gains = jnp.concatenate([gain_in[i][:, :share] for i in range(gain_in.shape[0])], axis=1)
-    gains = jnp.concatenate([gains] * (LANES // gains.shape[0]), axis=0).T
+    gains = jnp.concatenate([gain_in[i] for i in range(gain_in.shape[0])], axis=1)
+    pad_buf[:degrees, :LANES] = gains
+    gains = pad_buf[:, :LANES].T
     for deg in range(degrees):
         gain_b[deg] = jnp.broadcast_to(gains[:, deg:deg + 1], (LANES, LANES))
 
@@ -179,24 +203,35 @@
 
         lax.fori_loop(1, coefs, up_step, 0, unroll=4)
 
-        def grid_step(j, carry):
-            span = pl.ds(pl.multiple_of(j * STEP, 8), STEP)
-            y_j = jnp.concatenate([y0[span, :], y1[span, :]], axis=1).astype(BF16)
-            dm_j = jnp.concatenate([z0[span, :], z1[span, :]], axis=1).astype(BF16)
-            u = mm(tt_ref[...], y_j).astype(BF16).astype(F32)
-            sig = sigmoid(u)
-            act = u * sig
-            z_j = mm(ft_ref[...], act.astype(BF16))
-            z0[span, :] = z_j[:, :LANES]
-            z1[span, :] = z_j[:, LANES:]
-            ds = mm(f_ref[...], dm_j).astype(BF16).astype(F32)
-            du = (ds * (sig + act * (1.0 - sig))).astype(BF16)
-            dy_j = mm(t_ref[...], du)
-            y0[span, :] = dy_j[:, :LANES]
-            y1[span, :] = dy_j[:, LANES:]
+        groups = LANES // WIDE
+
+        def spans_of(group):
+            return [pl.ds(pl.multiple_of((group * WIDE + i) * STEP, 8), STEP) for i in range(WIDE)]
+
+        def grid_step(i, carry):
+            late = spans_of(jnp.maximum(i - 2, 0))
+            early = spans_of(jnp.minimum(i, groups - 1))
+            ys = [jnp.concatenate([y0[span, :], y1[span, :]], axis=1).astype(BF16) for span in early]
+            dms = [jnp.concatenate([z0[span, :], z1[span, :]], axis=1).astype(BF16) for span in early]
+            zs = [mm(ft_ref[...], act_buf[n]) for n in range(WIDE)]
+            dys = [mm(t_ref[...], du_buf[n]) for n in range(WIDE)]
+            for n in range(WIDE):
+                half = u_buf[n].astype(F32)
+                tan = jnp.tanh(half)
+                both = half * tan
+                act_buf[n] = (half + both).astype(BF16)
+                du_buf[n] = (s_buf[n].astype(F32) * ((1.0 + tan) + (half - both * tan))).astype(BF16)
+            for n in range(WIDE):
+                u_buf[n] = mm(tt_ref[...], ys[n]).astype(BF16)
+                s_buf[n] = mm(f_ref[...], dms[n]).astype(BF16)
+            for span, z_j, dy_j in zip(late, zs, dys):
+                z0[span, :] = z_j[:, :LANES]
+                z1[span, :] = z_j[:, LANES:]
+                y0[span, :] = dy_j[:, :LANES]
+                y1[span, :] = dy_j[:, LANES:]
             return carry
 
-        lax.fori_loop(0, LANES, grid_step, 0, unroll=2)
+        lax.fori_loop(0, groups + 2, grid_step, 0)
 
         def hidden_grad(k):
             picked = pl.ds(k, LANES, stride=STEP)
@@ -211,10 +246,10 @@
         d_pre = (dm_zero * (sig + gate * (1.0 - sig))).astype(BF16)
         gate = gate.astype(BF16)
         o_buf[chunk, 0] = (x_buf[chunk, 0].astype(F32) + mm(wdt[0], gate)).astype(BF16)
-        gdown_ref[0] += mm_nt(gate, g_zero)
+        g_sum[degrees] += mm_nt(gate, g_zero)
         dy_zero = hidden_grad(0)
-        gup_ref[0] += mm_nt(dy_zero, n_zero)
-        ggate_ref[...] += mm_nt(d_pre, n_zero)
+        g_sum[0] += mm_nt(dy_zero, n_zero)
+        g_sum[2 * degrees] += mm_nt(d_pre, n_zero)
         dn_zero = (mm(wut[0], dy_zero) + mm(wgt[...], d_pre)).astype(BF16).astype(F32)
 
         def down_step(k, acc):
@@ -224,16 +259,14 @@
             dy_k = hidden_grad(k)
             x_k = x_buf[chunk, k].astype(F32)
             o_buf[chunk, k] = (x_k + mm(wdt[deg], m_k)).astype(BF16)
-            gdown_ref[deg] += mm_nt(m_k, g_buf[chunk, k])
+            g_sum[degrees + deg] += mm_nt(m_k, g_buf[chunk, k])
             dn_k = mm(wut[deg], dy_k).astype(BF16)
             dn_buf[k] = dn_k
-            gup_ref[deg] += mm_nt(dy_k, n_buf[k])
+            g_sum[deg] += mm_nt(dy_k, n_buf[k])
             return acc + dn_k.astype(F32) * gain_b[deg] * x_k
 
         dot_v = lax.fori_loop(1, coefs, down_step, jnp.zeros((LANES, LANES), F32), unroll=4)
-        for flip in (2, 3, 1):
-            output_copy(0, chunk, flip).start()
-        output_local(0, chunk).start()
+        start_outputs(0, chunk)
 
         z0[pl.ds(0, LANES, stride=STEP), :] = blank
         z1[pl.ds(0, LANES, stride=STEP), :] = blank
@@ -251,12 +284,68 @@
             return carry
 
         lax.fori_loop(1, coefs, back_step, 0, unroll=4)
-        for flip in (2, 3, 1):
-            output_copy(1, chunk, flip).start()
-        output_local(1, chunk).start()
+        start_outputs(1, chunk)
         return carry
 
     lax.fori_loop(0, chunks, chunk_step, 0)
+
+    hid = up_hbm.shape[1]
+    part = hid // 2
+    slices = half_buf.shape[0]
+
+    def sum_rows(who, where):
+        return pl.ds(pl.multiple_of(who * hid + where * part, part), part)
+
+    def push(src, dst, num, peer):
+        return pltpu.make_async_remote_copy(src, dst, r_send.at[num], r_recv.at[num], device_id=peer, device_id_type=MESH)
+
+    halves = [push(g_sum.at[:, sum_rows(n, 1 - side), :], half_buf.at[n], n, {'dp': 1 - side}) for n in range(slices)]
+    for copy in halves:
+        copy.start()
+    for copy in halves:
+        copy.wait_recv()
+    rows_all = g_sum.shape[0]
+
+    def add_half(row, carry):
+        for n in range(slices):
+            half_buf[n, row] += g_sum[row, sum_rows(n, side), :]
+        return carry
+
+    lax.fori_loop(0, rows_all, add_half, 0)
+    shares = [push(half_buf.at[mate], mate_buf.at[0], slices, {'tp': mate}),
+              push(half_buf.at[mate ^ 2], mate_buf.at[1], slices + 1, {'tp': mate})]
+    for copy in shares:
+        copy.start()
+    for copy in shares:
+        copy.wait()
+
+    def add_mate(row, carry):
+        mate_buf[0, row] += half_buf[me, row]
+        mate_buf[1, row] += half_buf[me ^ 2, row]
+        return carry
+
+    lax.fori_loop(0, rows_all, add_mate, 0)
+    cross = push(mate_buf.at[1], far_buf, slices + 2, {'tp': me ^ 2})
+    cross.start()
+    for tensor in (0, 1):
+        for flip in (2, 3):
+            output_copy(tensor, chunks - 1, flip).start()
+    cross.wait()
+    mine = pl.ds(pl.multiple_of(side * part, part), part)
+
+    def add_far(row, carry):
+        fin_buf[row, mine, :] = (mate_buf[0, row] + far_buf[row]).astype(BF16)
+        return carry
+
+    lax.fori_loop(0, rows_all, add_far, 0)
+    last = push(fin_buf.at[:, mine, :], fin_buf.at[:, mine, :], slices + 3, {'dp': 1 - side})
+    last.start()
+    last.wait()
+    for copy in halves:
+        copy.wait_send()
+    dup_ref[...] = fin_buf[:degrees]
+    ddown_ref[...] = fin_buf[degrees:2 * degrees]
+    dgate_ref[...] = fin_buf[2 * degrees]
 
     def finish(chunk, carry):
         for tensor in (0, 1):
@@ -286,45 +375,44 @@
         g_t = jnp.transpose(grad_loc, (1, 2, 0))
         up_t = jnp.transpose(up_loc, (0, 2, 1))
         gate_t = jnp.transpose(gate_loc, (1, 0))
-        gain_pad = jnp.pad(gain_loc, ((0, 8 - degrees), (0, LANES - share)))
-        t_pad = jnp.pad(to_grid.astype(BF16), ((0, STEP - coefs), (0, pts - points)))
-        f_pad = jnp.pad(from_grid.astype(BF16), ((0, pts - points), (1, STEP - coefs)))
         hbm = pl.BlockSpec(memory_space=pl.ANY)
         vmem = pl.BlockSpec(memory_space=pltpu.VMEM)
         dma = pltpu.SemaphoreType.DMA
         act = (chunks, coefs, channels, LANES)
         wide = pltpu.VMEM((LANES * STEP, LANES), F32)
-        out_t, dx_t, g_up, g_gate, g_down = pl.pallas_call(
+        pair = pltpu.VMEM((WIDE, pts, 2 * LANES), BF16)
+        out_t, dx_t, d_up, d_gate, d_down = pl.pallas_call(
             fused_kernel,
             out_shape=(
                 jax.ShapeDtypeStruct(x_t.shape, BF16),
                 jax.ShapeDtypeStruct(x_t.shape, BF16),
-                jax.ShapeDtypeStruct((degrees, hidden, channels), F32),
-                jax.ShapeDtypeStruct((hidden, channels), F32),
-                jax.ShapeDtypeStruct((degrees, hidden, channels), F32)),
-            in_specs=[hbm] * 6 + [vmem] * 4,
+                jax.ShapeDtypeStruct((degrees, hid, channels), BF16),
+                jax.ShapeDtypeStruct((hid, channels), BF16),
+                jax.ShapeDtypeStruct((degrees, hid, channels), BF16)),
+            in_specs=[hbm] * 6 + [vmem] * 2,
             out_specs=(hbm, hbm, vmem, vmem, vmem),
             scratch_shapes=[
                 pltpu.VMEM(act, BF16), pltpu.VMEM(act, BF16), pltpu.VMEM(act, BF16),
                 pltpu.VMEM(act[1:], BF16), pltpu.VMEM(act[1:], BF16),
                 wide, wide, wide, wide,
                 pltpu.VMEM((degrees, hidden, channels), BF16), pltpu.VMEM((hidden, channels), BF16),
-                pltpu.VMEM((degrees, hidden, channels), BF16), pltpu.VMEM((tp_size, 8, LANES), F32),
+                pltpu.VMEM((degrees, hidden, channels), BF16), pltpu.VMEM((tp_size, degrees, share), F32),
                 pltpu.VMEM((degrees, channels, hidden), BF16), pltpu.VMEM((channels, hidden), BF16),
                 pltpu.VMEM((degrees, channels, hidden), BF16), pltpu.VMEM((degrees, channels, LANES), F32),
+                pltpu.VMEM((pts, STEP), BF16), pltpu.VMEM((STEP, pts), BF16), pltpu.VMEM((pts, STEP), BF16), pltpu.VMEM((STEP, pts), BF16),
+                pltpu.VMEM((LANES, 2 * LANES), F32), pair, pair, pair, pair,
+                pltpu.VMEM((2 * degrees + 1, hidden, channels), F32), pltpu.VMEM((tp_size, 2 * degrees + 1, hid // 2, channels), F32),
+                pltpu.VMEM((2, 2 * degrees + 1, hid // 2, channels), F32), pltpu.VMEM((2 * degrees + 1, hid // 2, channels), F32),
+                pltpu.VMEM((2 * degrees + 1, hid, channels), BF16),
                 dma((4, 4)), dma((4, 4)), dma((4,)),
                 dma((2, chunks, 4)), dma((2, chunks, 4)), dma((2, chunks)),
-                dma((2, chunks, 4)), dma((2, chunks, 4)), dma((2, chunks))],
+                dma((2, chunks, 4)), dma((2, chunks, 4)), dma((2, chunks)),
+                dma((tp_size + 4,)), dma((tp_size + 4,))],
             compiler_params=pltpu.CompilerParams(collective_id=0, has_side_effects=True, vmem_limit_bytes=62 * 1024 * 1024),
             name='fused',
-        )(x_t, g_t, up_t, gate_t, down_loc, gain_pad, t_pad.T, t_pad, f_pad, f_pad.T)
+        )(x_t, g_t, up_t, gate_t, down_loc, gain_loc, to_grid, jnp.transpose(from_grid, (1, 0)))
         back = lambda val: jnp.transpose(val, (2, 0, 1))
 
-        def reduce(val, dim):
-            return lax.psum(lax.psum_scatter(val, 'tp', scatter_dimension=dim, tiled=True), 'dp').astype(BF16)
-
-        d_up = jnp.transpose(reduce(g_up, 1), (0, 2, 1))
-        d_gate = jnp.transpose(reduce(g_gate, 0), (1, 0))
-        return back(out_t), back(dx_t), d_up, d_gate, reduce(g_down, 1)
+        return back(out_t), back(dx_t), jnp.transpose(d_up, (0, 2, 1)), jnp.transpose(d_gate, (1, 0)), d_down
 
     return jax.shard_map(local_step, mesh=mesh, in_specs=in_specs, out_specs=out_specs, check_vma=False)

time: 478 us -> 306 us (0.64)
  Pallas kernels: 375 us -> 293 us
  waiting for transfers between devices: 56 us -> 0 us
  blocking collectives: 17.3 us -> 0 us
  between operations: 13.8 us -> 0.66 us
    pallas_call x1, Pallas kernels: 375 us -> 293 us  [local_step(): pl.pallas_call(fused_kernel, out_shape=(jax.ShapeDtypeStruct(x_t.shape, B...]
    reduce_scatter x3 -> x0, waiting for transfers between devices: 54.6 us -> none  [reduce(): lax.psum_scatter(val, 'tp', scatter_dimension=dim, tiled=True)]
    psum x1 -> x0, blocking collectives: 17.3 us -> none  [reduce(): lax.psum(lax.psum_scatter(val, 'tp', scatter_dimension=dim, tiled=True),...]
    unnamed x7 -> x13, local copies, waits for them, and re-layouts: 9.74 us -> 11.5 us
  transfers between devices with their start and end apart: 3 -> 0, of which waited for: 3 -> 0; matrix products, arithmetic and copies ran while one was open for 0% -> 0% of each run, Pallas kernels for 0% -> 0%
where the time goes in v2:
time: 306 us
  Pallas kernels  293 us (96%)
  local copies, waits for them, and re-layouts  11.5 us (4%)
    pallas_call x1, Pallas kernels, local_step(): pl.pallas_call(fused_kernel, out_shape=(jax.ShapeDtypeStruct(x_t.shape, B...  293 us
    unnamed x13, local copies, waits for them, and re-layouts  11.5 us

profile of v2, /device:TPU:0, one launch (start us, length us, event | category | flops | bytes accessed | tf_op | source)
XLA Modules:
  0.0 305.5 jit_solution(10266346337046813098)
XLA Ops:
  0.6 293.3 %fused.1 = (bf16[49,32,2048]{2,1,0:T(8,128)(2,1)}, bf16[49,32,2048]{2,1,0:T(8,128)(2,1)}, bf16[7,64,128]{2,1,0:T(8,128)(2,1)}, bf16[64,128]{1,0:T(8,128)(2,1)}, bf16[7,64,128]{2,1,0:T(8,128)(2,1)}) custom-call(bf16[49,32,2048]{2,1,0:T(8,128)(2,1)} %bitcast.9, bf16[49,32,2048]{2,1,0:T(8,128)(2,1)} %bitcast.10, bf16[7,64,128]{2,1,0:T(8,128)(2,1)} %bitcast.13, ...), custom_call_target="tpu_custom_call" | custom-call | tf_op jit(solution)/shard_map/fused/pallas_call | solution.py:384
  294.0 0.0 copy-start
  294.0 6.9 %copy.18 = bf16[2048,49,32]{0,2,1:T(8,128)(2,1)} copy(bf16[2048,49,32]{0,2,1:T(8,128)(2,1)} %bitcast.12) | data formatting | bytes 12845056
  300.9 0.0 copy-done
  300.9 0.0 copy-start.2
  300.9 0.0 copy-start.3
  300.9 0.0 copy-start.1
  300.9 2.7 copy.19
  303.6 0.0 copy-done.2
  303.6 0.6 copy.20
  304.3 0.0 copy-done.3
  304.3 0.6 copy.21
  304.9 0.0 copy-done.1
  304.9 0.6 copy.22
Async XLA Ops:
  294.0 6.9 %copy-start = (bf16[49,32,2048]{2,1,0:T(8,128)(2,1)S(1)}, bf16[49,32,2048]{2,1,0:T(8,128)(2,1)}, u32[]{:S(2)}) copy-start(bf16[49,32,2048]{2,1,0:T(8,128)(2,1)} %get-tuple-element.11) | copy-start | bytes 19267588
  300.9 2.8 copy-start.2
  300.9 3.4 %copy-start.3 = (bf16[64,128]{1,0:T(8,128)(2,1)S(1)}, bf16[64,128]{1,0:T(8,128)(2,1)}, u32[]{:S(2)}) copy-start(bf16[64,128]{1,0:T(8,128)(2,1)} %get-tuple-element.13) | copy-start | bytes 49156
  300.9 4.0 %copy-start.1 = (bf16[7,64,128]{2,1,0:T(8,128)(2,1)S(1)}, bf16[7,64,128]{2,1,0:T(8,128)(2,1)}, u32[]{:S(2)}) copy-start(bf16[7,64,128]{2,1,0:T(8,128)(2,1)} %get-tuple-element.24) | copy-start | bytes 344068

commit v3 on v2

--- a/solution.py
+++ b/solution.py
@@ -33,13 +33,13 @@
     return 0.5 * jnp.tanh(0.5 * val) + 0.5
 
 
-def fused_kernel(x_hbm, g_hbm, up_hbm, gate_hbm, down_hbm, gain_hbm, tg_ref, fg_ref,
-                 out_hbm, dx_hbm, dup_ref, dgate_ref, ddown_ref,
+def fused_kernel(x_hbm, g_hbm, up_hbm, gate_hbm, down_hbm, gain_hbm, tg_hbm, fg_hbm,
+                 out_vm, dx_vm, fin_vm,
                  x_buf, g_buf, o_buf, n_buf, dn_buf, y0, y1, z0, z1,
                  wu, wg, wd, gain_in, wut, wgt, wdt, gain_b,
                  tt_ref, t_ref, f_ref, ft_ref, pad_buf, u_buf, s_buf, act_buf, du_buf,
                  g_sum, half_buf, mate_buf, far_buf, fin_buf,
-                 w_send, w_recv, w_loc, in_send, in_recv, in_loc, o_send, o_recv, o_loc, r_send, r_recv):
+                 tg_ref, fg_ref, w_send, w_recv, w_loc, in_send, in_recv, in_loc, o_send, o_recv, r_send, r_recv):
     chunks, coefs = x_buf.shape[0], x_buf.shape[1]
     share = x_hbm.shape[1]
     own = chunks * LANES
@@ -57,7 +57,8 @@
     for flip in (1, 2, 3):
         pl.semaphore_signal(barrier, inc=1, device_id={'tp': me ^ flip}, device_id_type=MESH)
     pl.semaphore_signal(barrier, inc=1, device_id={'dp': 1 - side}, device_id_type=MESH)
-    pl.semaphore_wait(barrier, 4)
+    pl.semaphore_signal(barrier, inc=1, device_id={'dp': 1 - side, 'tp': mate}, device_id_type=MESH)
+    pl.semaphore_wait(barrier, 5)
 
     def weight_parts(who):
         hid = up_hbm.shape[1]
@@ -65,20 +66,25 @@
 
     sources = (up_hbm, down_hbm, gate_hbm, gain_hbm)
 
-    def weight_copies(flip):
-        if flip == 3:
-            parts = weight_parts(me ^ 2)
-            pairs = zip(parts, parts)
-            peer = mate
-        else:
-            pairs = zip(sources, weight_parts(me))
-            peer = me ^ flip
-        return [pltpu.make_async_remote_copy(src, dst, w_send.at[flip, i], w_recv.at[flip, i], device_id={'tp': peer}, device_id_type=MESH)
-                for i, (src, dst) in enumerate(pairs)]
-
-    own_weights = [pltpu.make_async_copy(src, dst, w_loc.at[i]) for i, (src, dst) in enumerate(zip(sources, weight_parts(me)))]
-    far_weights, mate_weights, relay_weights = weight_copies(2), weight_copies(1), weight_copies(3)
-    for copy in far_weights + mate_weights + own_weights:
+    def weight_copies(srcs, dsts, num, to, peer):
+        return [pltpu.make_async_remote_copy(src, dst, w_send.at[to, i], w_recv.at[num, i], device_id=peer, device_id_type=MESH)
+                for i, (src, dst) in enumerate(zip(srcs, dsts))]
+
+    crosses = lax.rem(me, 2) == side
+    mine, far = weight_parts(me), weight_parts(me ^ 2)
+    own_weights = [pltpu.make_async_copy(src, dst, w_loc.at[i]) for i, (src, dst) in enumerate(zip(sources, mine))]
+    far_weights = weight_copies(sources, mine, 2, 0, {'tp': me ^ 2})
+    mate_weights = weight_copies(sources, mine, 1, 1, {'tp': mate})
+    passed_weights = (weight_copies(far, far, 3, 2, {'tp': mate}) + weight_copies(far, far, 2, 3, {'dp': 1 - side})
+                      + weight_copies(far, far, 3, 4, {'dp': 1 - side, 'tp': mate}))
+    grids = [pltpu.make_async_copy(tg_hbm, tg_ref, w_loc.at[4]), pltpu.make_async_copy(fg_hbm, fg_ref, w_loc.at[5])]
+
+    @pl.when(crosses)
+    def _():
+        for copy in far_weights:
+            copy.start()
+
+    for copy in mate_weights + own_weights + grids:
         copy.start()
 
     def input_copy(tensor, chunk, flip):
@@ -93,15 +99,15 @@
         return pltpu.make_async_copy(src.at[:, :, lanes(me, chunk)], buf.at[chunk, :, rows(me, share), :], in_loc.at[tensor, chunk])
 
     def output_copy(tensor, chunk, flip):
-        buf, dst = ((o_buf, out_hbm), (g_buf, dx_hbm))[tensor]
+        buf, dst = ((o_buf, out_vm), (g_buf, dx_vm))[tensor]
         return pltpu.make_async_remote_copy(
             buf.at[chunk, :, rows(me ^ flip, share), :], dst.at[:, :, lanes(me, chunk)],
             o_send.at[tensor, chunk, flip], o_recv.at[tensor, chunk, flip],
             device_id={'tp': me ^ flip}, device_id_type=MESH)
 
     def output_local(tensor, chunk):
-        buf, dst = ((o_buf, out_hbm), (g_buf, dx_hbm))[tensor]
-        return pltpu.make_async_copy(buf.at[chunk, :, rows(me, share), :], dst.at[:, :, lanes(me, chunk)], o_loc.at[tensor, chunk])
+        buf, dst = ((o_buf, out_vm), (g_buf, dx_vm))[tensor]
+        dst[:, :, lanes(me, chunk)] = buf[chunk, :, rows(me, share), :]
 
     def start_outputs(tensor, chunk):
         @pl.when(chunk < chunks - 1)
@@ -110,7 +116,7 @@
                 output_copy(tensor, chunk, flip).start()
 
         output_copy(tensor, chunk, 1).start()
-        output_local(tensor, chunk).start()
+        output_local(tensor, chunk)
 
     def start_inputs(chunk, carry):
         for flip in (2, 3, 1):
@@ -130,6 +136,8 @@
     for ref in (z0, z1):
         ref[pl.ds(0, LANES, stride=STEP), :] = blank
 
+    for copy in grids:
+        copy.wait()
     points = tg_ref.shape[1]
     pts = t_ref.shape[1]
     pad_buf[...] = jnp.zeros_like(pad_buf)
@@ -141,12 +149,19 @@
     ft_ref[...] = pad_buf[:STEP, :pts].astype(BF16)
     f_ref[...] = (0.5 * pad_buf[...]).T[:pts, :STEP].astype(BF16)
 
-    for far, relay in zip(far_weights, relay_weights):
-        far.wait_recv()
-        relay.start()
     for copy in far_weights:
-        copy.wait_send()
-    for copy in mate_weights + relay_weights + own_weights:
+        copy.wait_recv()
+
+    @pl.when(crosses)
+    def _():
+        for copy in passed_weights:
+            copy.start()
+        for copy in far_weights + passed_weights:
+            copy.wait_send()
+
+    for copy in passed_weights[:len(sources)]:
+        copy.wait_recv()
+    for copy in mate_weights + own_weights:
         copy.wait()
 
     def turn(deg, carry):
@@ -331,31 +346,45 @@
         for flip in (2, 3):
             output_copy(tensor, chunks - 1, flip).start()
     cross.wait()
-    mine = pl.ds(pl.multiple_of(side * part, part), part)
+    ours = pl.ds(pl.multiple_of(side * part, part), part)
 
     def add_far(row, carry):
-        fin_buf[row, mine, :] = (mate_buf[0, row] + far_buf[row]).astype(BF16)
+        fin_buf[row, ours, :] = (mate_buf[0, row] + far_buf[row]).astype(BF16)
         return carry
 
     lax.fori_loop(0, rows_all, add_far, 0)
-    last = push(fin_buf.at[:, mine, :], fin_buf.at[:, mine, :], slices + 3, {'dp': 1 - side})
+    last = push(fin_buf.at[:, ours, :], fin_buf.at[:, ours, :], slices + 3, {'dp': 1 - side})
     last.start()
     last.wait()
     for copy in halves:
         copy.wait_send()
-    dup_ref[...] = fin_buf[:degrees]
-    ddown_ref[...] = fin_buf[degrees:2 * degrees]
-    dgate_ref[...] = fin_buf[2 * degrees]
+    fin_vm[...] = fin_buf[...]
 
     def finish(chunk, carry):
         for tensor in (0, 1):
             for flip in (2, 3, 1):
                 input_copy(tensor, chunk, flip).wait_send()
                 output_copy(tensor, chunk, flip).wait()
-            output_local(tensor, chunk).wait()
         return carry
 
     lax.fori_loop(0, chunks, finish, 0)
+
+
+def write_kernel(out_vm, dx_vm, fin_vm, out_hbm, dx_hbm, dup_hbm, dgate_hbm, ddown_hbm, sems, small):
+    coefs, step = out_hbm.shape[0], 7
+    degrees = dup_hbm.shape[0]
+    copies = []
+    for start in range(0, coefs, step):
+        span = pl.ds(start, step)
+        copies.append(pltpu.make_async_copy(out_vm.at[span], out_hbm.at[span], sems.at[0, start]))
+        copies.append(pltpu.make_async_copy(dx_vm.at[span], dx_hbm.at[span], sems.at[1, start]))
+    copies.append(pltpu.make_async_copy(fin_vm.at[pl.ds(0, degrees)], dup_hbm, small.at[0]))
+    copies.append(pltpu.make_async_copy(fin_vm.at[pl.ds(degrees, degrees)], ddown_hbm, small.at[1]))
+    copies.append(pltpu.make_async_copy(fin_vm.at[2 * degrees], dgate_hbm, small.at[2]))
+    for copy in copies:
+        copy.start()
+    for copy in copies:
+        copy.wait()
 
 
 def solution(mesh):
@@ -381,16 +410,11 @@
         act = (chunks, coefs, channels, LANES)
         wide = pltpu.VMEM((LANES * STEP, LANES), F32)
         pair = pltpu.VMEM((WIDE, pts, 2 * LANES), BF16)
-        out_t, dx_t, d_up, d_gate, d_down = pl.pallas_call(
+        out_v, dx_v, fin_v = pl.pallas_call(
             fused_kernel,
-            out_shape=(
-                jax.ShapeDtypeStruct(x_t.shape, BF16),
-                jax.ShapeDtypeStruct(x_t.shape, BF16),
-                jax.ShapeDtypeStruct((degrees, hid, channels), BF16),
-                jax.ShapeDtypeStruct((hid, channels), BF16),
-                jax.ShapeDtypeStruct((degrees, hid, channels), BF16)),
-            in_specs=[hbm] * 6 + [vmem] * 2,
-            out_specs=(hbm, hbm, vmem, vmem, vmem),
+            out_shape=(pltpu.VMEM(x_t.shape, BF16), pltpu.VMEM(x_t.shape, BF16), pltpu.VMEM((2 * degrees + 1, hid, channels), BF16)),
+            in_specs=[hbm] * 8,
+            out_specs=(vmem, vmem, vmem),
             scratch_shapes=[
                 pltpu.VMEM(act, BF16), pltpu.VMEM(act, BF16), pltpu.VMEM(act, BF16),
                 pltpu.VMEM(act[1:], BF16), pltpu.VMEM(act[1:], BF16),
@@ -404,15 +428,29 @@
                 pltpu.VMEM((2 * degrees + 1, hidden, channels), F32), pltpu.VMEM((tp_size, 2 * degrees + 1, hid // 2, channels), F32),
                 pltpu.VMEM((2, 2 * degrees + 1, hid // 2, channels), F32), pltpu.VMEM((2 * degrees + 1, hid // 2, channels), F32),
                 pltpu.VMEM((2 * degrees + 1, hid, channels), BF16),
-                dma((4, 4)), dma((4, 4)), dma((4,)),
+                pltpu.VMEM(to_grid.shape, F32), pltpu.VMEM(from_grid.shape[::-1], F32),
+                dma((5, 4)), dma((4, 4)), dma((6,)),
                 dma((2, chunks, 4)), dma((2, chunks, 4)), dma((2, chunks)),
-                dma((2, chunks, 4)), dma((2, chunks, 4)), dma((2, chunks)),
+                dma((2, chunks, 4)), dma((2, chunks, 4)),
                 dma((tp_size + 4,)), dma((tp_size + 4,))],
-            compiler_params=pltpu.CompilerParams(collective_id=0, has_side_effects=True, vmem_limit_bytes=62 * 1024 * 1024),
+            compiler_params=pltpu.CompilerParams(collective_id=0, has_side_effects=True, vmem_limit_bytes=48 * 1024 * 1024),
             name='fused',
         )(x_t, g_t, up_t, gate_t, down_loc, gain_loc, to_grid, jnp.transpose(from_grid, (1, 0)))
+        out_t, dx_t, d_up, d_gate, d_down = pl.pallas_call(
+            write_kernel,
+            out_shape=(
+                jax.ShapeDtypeStruct(x_t.shape, BF16),
+                jax.ShapeDtypeStruct(x_t.shape, BF16),
+                jax.ShapeDtypeStruct((degrees, hid, channels), BF16),
+                jax.ShapeDtypeStruct((hid, channels), BF16),
+                jax.ShapeDtypeStruct((degrees, hid, channels), BF16)),
+            in_specs=[vmem] * 3,
+            out_specs=(hbm,) * 5,
+            scratch_shapes=[dma((2, coefs)), dma((3,))],
+            compiler_params=pltpu.CompilerParams(vmem_limit_bytes=1024 * 1024),
+            name='write',
+        )(out_v, dx_v, fin_v)
         back = lambda val: jnp.transpose(val, (2, 0, 1))
-
         return back(out_t), back(dx_t), jnp.transpose(d_up, (0, 2, 1)), jnp.transpose(d_gate, (1, 0)), d_down
 
     return jax.shard_map(local_step, mesh=mesh, in_specs=in_specs, out_specs=out_specs, check_vma=False)

time: 306 us -> 296 us (0.967)
  local copies, waits for them, and re-layouts: 11.5 us -> 0 us
    unnamed x13 -> x0, local copies, waits for them, and re-layouts: 11.5 us -> none
    pallas_call x1 -> x2, Pallas kernels: 293 us -> 294 us  [the longest x1 289 us: local_step(): pl.pallas_call(fused_kernel, out_shape=(pltpu.VMEM(x_t.shape, BF16), pltp...]
where the time goes in v3:
time: 296 us; the launch traced here: 295 us
  Pallas kernels  294 us (99%)
    pallas_call x1, Pallas kernels, local_step(): pl.pallas_call(fused_kernel, out_shape=(pltpu.VMEM(x_t.shape, BF16), pltp...  289 us

profile of v3, /device:TPU:0, one launch (start us, length us, event | category | flops | bytes accessed | tf_op | source)
XLA Modules:
  0.0 295.1 jit_solution(15176755102502791470)
XLA Ops:
  0.6 288.8 %fused.1 = (bf16[49,32,2048]{2,1,0:T(8,128)(2,1)S(1)}, bf16[49,32,2048]{2,1,0:T(8,128)(2,1)S(1)}, bf16[15,64,128]{2,1,0:T(8,128)(2,1)S(1)}) custom-call(bf16[49,32,2048]{2,1,0:T(8,128)(2,1)} %bitcast.9, bf16[49,32,2048]{2,1,0:T(8,128)(2,1)} %bitcast.10, bf16[7,64,128]{2,1,0:T(8,128)(2,1)} %bitcast.11, bf16[64,128]{1,0:T(8,128)(2,1)} %bitcast.13, ...), custom_call_target="tpu_custom_call" | custom-call | tf_op jit(solution)/shard_map/fused/pallas_call | solution.py:413
  289.5 5.6 %write.1 = (bf16[49,32,2048]{2,1,0:T(8,128)(2,1)}, bf16[49,32,2048]{2,1,0:T(8,128)(2,1)}, bf16[7,64,128]{2,1,0:T(8,128)(2,1)}, bf16[64,128]{1,0:T(8,128)(2,1)}, bf16[7,64,128]{2,1,0:T(8,128)(2,1)}) custom-call(bf16[49,32,2048]{2,1,0:T(8,128)(2,1)S(1)} %get-tuple-element.13.out_vm, bf16[49,32,2048]{2,1,0:T(8,128)(2,1)S(1)} %get-tuple-element.14.dx_vm, ...), custom_call_target="tpu_custom_call" | custom-call | tf_op jit(solution)/shard_map/write/pallas_call | solution.py:439

commit v4 on v3

--- a/solution.py
+++ b/solution.py
@@ -39,7 +39,7 @@
                  wu, wg, wd, gain_in, wut, wgt, wdt, gain_b,
                  tt_ref, t_ref, f_ref, ft_ref, pad_buf, u_buf, s_buf, act_buf, du_buf,
                  g_sum, half_buf, mate_buf, far_buf, fin_buf,
-                 tg_ref, fg_ref, w_send, w_recv, w_loc, in_send, in_recv, in_loc, o_send, o_recv, r_send, r_recv):
+                 tg_ref, fg_ref, w_send, w_recv, w_loc, in_send, in_recv, o_send, o_recv, r_send, r_recv):
     chunks, coefs = x_buf.shape[0], x_buf.shape[1]
     share = x_hbm.shape[1]
     own = chunks * LANES
@@ -53,6 +53,9 @@
     def lanes(who, chunk):
         return pl.ds(pl.multiple_of(who * own + chunk * LANES, LANES), LANES)
 
+    def drain(ref, sem):
+        pltpu.make_async_copy(ref, ref, sem).wait()
+
     barrier = pltpu.get_barrier_semaphore()
     for flip in (1, 2, 3):
         pl.semaphore_signal(barrier, inc=1, device_id={'tp': me ^ flip}, device_id_type=MESH)
@@ -66,18 +69,20 @@
 
     sources = (up_hbm, down_hbm, gate_hbm, gain_hbm)
 
-    def weight_copies(srcs, dsts, num, to, peer):
-        return [pltpu.make_async_remote_copy(src, dst, w_send.at[to, i], w_recv.at[num, i], device_id=peer, device_id_type=MESH)
+    def weight_copies(srcs, dsts, come, to, peer):
+        return [pltpu.make_async_remote_copy(src, dst, w_send.at[to, i], w_recv.at[come, i], device_id=peer, device_id_type=MESH)
                 for i, (src, dst) in enumerate(zip(srcs, dsts))]
 
     crosses = lax.rem(me, 2) == side
     mine, far = weight_parts(me), weight_parts(me ^ 2)
-    own_weights = [pltpu.make_async_copy(src, dst, w_loc.at[i]) for i, (src, dst) in enumerate(zip(sources, mine))]
-    far_weights = weight_copies(sources, mine, 2, 0, {'tp': me ^ 2})
+    own_weights = [pltpu.make_async_copy(src, dst, w_loc.at[0, i]) for i, (src, dst) in enumerate(zip(sources, mine))]
+    far_weights = weight_copies(sources, mine, 0, 0, {'tp': me ^ 2})
     mate_weights = weight_copies(sources, mine, 1, 1, {'tp': mate})
-    passed_weights = (weight_copies(far, far, 3, 2, {'tp': mate}) + weight_copies(far, far, 2, 3, {'dp': 1 - side})
-                      + weight_copies(far, far, 3, 4, {'dp': 1 - side, 'tp': mate}))
-    grids = [pltpu.make_async_copy(tg_hbm, tg_ref, w_loc.at[4]), pltpu.make_async_copy(fg_hbm, fg_ref, w_loc.at[5])]
+    passed_weights = (weight_copies(far, far, 2, 2, {'tp': mate}) + weight_copies(far, far, 0, 2, {'dp': 1 - side})
+                      + weight_copies(far, far, 2, 2, {'dp': 1 - side, 'tp': mate}))
+    hid = up_hbm.shape[1]
+    thrice = (wu.at[:, pl.ds(0, 3 * hid), :], wd.at[:, pl.ds(0, 3 * hid), :], wg.at[pl.ds(0, 3 * hid), :], gain_in.at[pl.ds(0, 3)])
+    grids = [pltpu.make_async_copy(tg_hbm, tg_ref, w_loc.at[1, 0]), pltpu.make_async_copy(fg_hbm, fg_ref, w_loc.at[1, 1])]
 
     @pl.when(crosses)
     def _():
@@ -91,18 +96,18 @@
         src, buf = ((x_hbm, x_buf), (g_hbm, g_buf))[tensor]
         return pltpu.make_async_remote_copy(
             src.at[:, :, lanes(me ^ flip, chunk)], buf.at[chunk, :, rows(me, share), :],
-            in_send.at[tensor, chunk, flip], in_recv.at[tensor, chunk, flip],
+            in_send.at[tensor], in_recv.at[tensor, chunk],
             device_id={'tp': me ^ flip}, device_id_type=MESH)
 
     def input_local(tensor, chunk):
         src, buf = ((x_hbm, x_buf), (g_hbm, g_buf))[tensor]
-        return pltpu.make_async_copy(src.at[:, :, lanes(me, chunk)], buf.at[chunk, :, rows(me, share), :], in_loc.at[tensor, chunk])
+        return pltpu.make_async_copy(src.at[:, :, lanes(me, chunk)], buf.at[chunk, :, rows(me, share), :], in_recv.at[tensor, chunk])
 
     def output_copy(tensor, chunk, flip):
         buf, dst = ((o_buf, out_vm), (g_buf, dx_vm))[tensor]
         return pltpu.make_async_remote_copy(
             buf.at[chunk, :, rows(me ^ flip, share), :], dst.at[:, :, lanes(me, chunk)],
-            o_send.at[tensor, chunk, flip], o_recv.at[tensor, chunk, flip],
+            o_send.at[tensor], o_recv.at[tensor],
             device_id={'tp': me ^ flip}, device_id_type=MESH)
 
     def output_local(tensor, chunk):
@@ -156,8 +161,9 @@
     def _():
         for copy in passed_weights:
             copy.start()
-        for copy in far_weights + passed_weights:
+        for i, copy in enumerate(far_weights):
             copy.wait_send()
+            drain(thrice[i], w_send.at[2, i])
 
     for copy in passed_weights[:len(sources)]:
         copy.wait_recv()
@@ -182,11 +188,8 @@
     inv_vec = 1.0 / (LANES * (coefs - 1))
 
     def chunk_step(chunk, carry):
-        for flip in (2, 3, 1):
-            for tensor in (0, 1):
-                input_copy(tensor, chunk, flip).wait_recv()
-        for tensor in (0, 1):
-            input_local(tensor, chunk).wait()
+        for tensor, buf in enumerate((x_buf, g_buf)):
+            drain(buf.at[chunk], in_recv.at[tensor, chunk])
 
         def square_sum(k, acc):
             val = x_buf[chunk, k].astype(F32)
@@ -304,7 +307,6 @@
 
     lax.fori_loop(0, chunks, chunk_step, 0)
 
-    hid = up_hbm.shape[1]
     part = hid // 2
     slices = half_buf.shape[0]
 
@@ -314,11 +316,9 @@
     def push(src, dst, num, peer):
         return pltpu.make_async_remote_copy(src, dst, r_send.at[num], r_recv.at[num], device_id=peer, device_id_type=MESH)
 
-    halves = [push(g_sum.at[:, sum_rows(n, 1 - side), :], half_buf.at[n], n, {'dp': 1 - side}) for n in range(slices)]
-    for copy in halves:
-        copy.start()
-    for copy in halves:
-        copy.wait_recv()
+    for n in range(slices):
+        push(g_sum.at[:, sum_rows(n, 1 - side), :], half_buf.at[n], 0, {'dp': 1 - side}).start()
+    drain(half_buf, r_recv.at[0])
     rows_all = g_sum.shape[0]
 
     def add_half(row, carry):
@@ -327,12 +327,10 @@
         return carry
 
     lax.fori_loop(0, rows_all, add_half, 0)
-    shares = [push(half_buf.at[mate], mate_buf.at[0], slices, {'tp': mate}),
-              push(half_buf.at[mate ^ 2], mate_buf.at[1], slices + 1, {'tp': mate})]
-    for copy in shares:
-        copy.start()
-    for copy in shares:
-        copy.wait()
+    push(half_buf.at[mate], mate_buf.at[0], 1, {'tp': mate}).start()
+    push(half_buf.at[mate ^ 2], mate_buf.at[1], 1, {'tp': mate}).start()
+    drain(mate_buf, r_recv.at[1])
+    drain(mate_buf, r_send.at[1])
 
     def add_mate(row, carry):
         mate_buf[0, row] += half_buf[me, row]
@@ -340,7 +338,7 @@
         return carry
 
     lax.fori_loop(0, rows_all, add_mate, 0)
-    cross = push(mate_buf.at[1], far_buf, slices + 2, {'tp': me ^ 2})
+    cross = push(mate_buf.at[1], far_buf, 2, {'tp': me ^ 2})
     cross.start()
     for tensor in (0, 1):
         for flip in (2, 3):
@@ -353,38 +351,35 @@
         return carry
 
     lax.fori_loop(0, rows_all, add_far, 0)
-    last = push(fin_buf.at[:, ours, :], fin_buf.at[:, ours, :], slices + 3, {'dp': 1 - side})
+    last = push(fin_buf.at[:, ours, :], fin_buf.at[:, ours, :], 3, {'dp': 1 - side})
     last.start()
     last.wait()
-    for copy in halves:
-        copy.wait_send()
+    drain(half_buf, r_send.at[0])
     fin_vm[...] = fin_buf[...]
 
-    def finish(chunk, carry):
-        for tensor in (0, 1):
-            for flip in (2, 3, 1):
-                input_copy(tensor, chunk, flip).wait_send()
-                output_copy(tensor, chunk, flip).wait()
-        return carry
-
-    lax.fori_loop(0, chunks, finish, 0)
-
-
-def write_kernel(out_vm, dx_vm, fin_vm, out_hbm, dx_hbm, dup_hbm, dgate_hbm, ddown_hbm, sems, small):
+    for tensor, (buf, dst) in enumerate(((o_buf, out_vm), (g_buf, dx_vm))):
+        sent = buf.at[:, :, pl.ds(0, LANES - share), :]
+        drain(sent, in_send.at[tensor])
+        drain(sent, o_send.at[tensor])
+        drain(dst.at[:, :, pl.ds(0, x_hbm.shape[2] - own)], o_recv.at[tensor])
+
+
+def write_kernel(out_vm, dx_vm, fin_vm, out_hbm, dx_hbm, dup_hbm, dgate_hbm, ddown_hbm, sems):
     coefs, step = out_hbm.shape[0], 7
     degrees = dup_hbm.shape[0]
-    copies = []
     for start in range(0, coefs, step):
         span = pl.ds(start, step)
-        copies.append(pltpu.make_async_copy(out_vm.at[span], out_hbm.at[span], sems.at[0, start]))
-        copies.append(pltpu.make_async_copy(dx_vm.at[span], dx_hbm.at[span], sems.at[1, start]))
-    copies.append(pltpu.make_async_copy(fin_vm.at[pl.ds(0, degrees)], dup_hbm, small.at[0]))
-    copies.append(pltpu.make_async_copy(fin_vm.at[pl.ds(degrees, degrees)], ddown_hbm, small.at[1]))
-    copies.append(pltpu.make_async_copy(fin_vm.at[2 * degrees], dgate_hbm, small.at[2]))
-    for copy in copies:
+        pltpu.make_async_copy(out_vm.at[span], out_hbm.at[span], sems.at[0]).start()
+        pltpu.make_async_copy(dx_vm.at[span], dx_hbm.at[span], sems.at[1]).start()
+    small = [pltpu.make_async_copy(fin_vm.at[pl.ds(0, degrees)], dup_hbm, sems.at[2]),
+             pltpu.make_async_copy(fin_vm.at[pl.ds(degrees, degrees)], ddown_hbm, sems.at[3]),
+             pltpu.make_async_copy(fin_vm.at[2 * degrees], dgate_hbm, sems.at[4])]
+    for copy in small:
         copy.start()
-    for copy in copies:
+    for copy in small:
         copy.wait()
+    pltpu.make_async_copy(out_vm, out_hbm, sems.at[0]).wait()
+    pltpu.make_async_copy(dx_vm, dx_hbm, sems.at[1]).wait()
 
 
 def solution(mesh):
@@ -429,10 +424,9 @@
                 pltpu.VMEM((2, 2 * degrees + 1, hid // 2, channels), F32), pltpu.VMEM((2 * degrees + 1, hid // 2, channels), F32),
                 pltpu.VMEM((2 * degrees + 1, hid, channels), BF16),
                 pltpu.VMEM(to_grid.shape, F32), pltpu.VMEM(from_grid.shape[::-1], F32),
-                dma((5, 4)), dma((4, 4)), dma((6,)),
-                dma((2, chunks, 4)), dma((2, chunks, 4)), dma((2, chunks)),
-                dma((2, chunks, 4)), dma((2, chunks, 4)),
-                dma((tp_size + 4,)), dma((tp_size + 4,))],
+                dma((3, 4)), dma((3, 4)), dma((2, 4)),
+                dma((2,)), dma((2, chunks)), dma((2,)), dma((2,)),
+                dma((4,)), dma((4,))],
             compiler_params=pltpu.CompilerParams(collective_id=0, has_side_effects=True, vmem_limit_bytes=48 * 1024 * 1024),
             name='fused',
         )(x_t, g_t, up_t, gate_t, down_loc, gain_loc, to_grid, jnp.transpose(from_grid, (1, 0)))
@@ -446,7 +440,7 @@
                 jax.ShapeDtypeStruct((degrees, hid, channels), BF16)),
             in_specs=[vmem] * 3,
             out_specs=(hbm,) * 5,
-            scratch_shapes=[dma((2, coefs)), dma((3,))],
+            scratch_shapes=[dma((5,))],
             compiler_params=pltpu.CompilerParams(vmem_limit_bytes=1024 * 1024),
             name='write',
         )(out_v, dx_v, fin_v)

time: 296 us -> 294 us (level)
  no operation moved by 1% of the time
where the time goes in v4:
time: 294 us; the launch traced here: 293 us
  Pallas kernels  292 us (99%)
    pallas_call x1, Pallas kernels, local_step(): pl.pallas_call(fused_kernel, out_shape=(pltpu.VMEM(x_t.shape, BF16), pltp...  288 us

profile of v4, /device:TPU:0, one launch (start us, length us, event | category | flops | bytes accessed | tf_op | source)
XLA Modules:
  0.0 293.0 jit_solution(14431264437262195199)
XLA Ops:
  0.6 287.6 %fused.1 = (bf16[49,32,2048]{2,1,0:T(8,128)(2,1)S(1)}, bf16[49,32,2048]{2,1,0:T(8,128)(2,1)S(1)}, bf16[15,64,128]{2,1,0:T(8,128)(2,1)S(1)}) custom-call(bf16[49,32,2048]{2,1,0:T(8,128)(2,1)} %bitcast.9, bf16[49,32,2048]{2,1,0:T(8,128)(2,1)} %bitcast.10, bf16[7,64,128]{2,1,0:T(8,128)(2,1)} %bitcast.11, bf16[64,128]{1,0:T(8,128)(2,1)} %bitcast.13, ...), custom_call_target="tpu_custom_call" | custom-call | tf_op jit(solution)/shard_map/fused/pallas_call | solution.py:408
  288.2 4.7 %write.1 = (bf16[49,32,2048]{2,1,0:T(8,128)(2,1)}, bf16[49,32,2048]{2,1,0:T(8,128)(2,1)}, bf16[7,64,128]{2,1,0:T(8,128)(2,1)}, bf16[64,128]{1,0:T(8,128)(2,1)}, bf16[7,64,128]{2,1,0:T(8,128)(2,1)}) custom-call(bf16[49,32,2048]{2,1,0:T(8,128)(2,1)S(1)} %get-tuple-element.13.out_vm, bf16[49,32,2048]{2,1,0:T(8,128)(2,1)S(1)} %get-tuple-element.14.dx_vm, ...), custom_call_target="tpu_custom_call" | custom-call | tf_op jit(solution)/shard_map/write/pallas_call | solution.py:433

commit v5 on v4

--- a/solution.py
+++ b/solution.py
@@ -39,7 +39,7 @@
                  wu, wg, wd, gain_in, wut, wgt, wdt, gain_b,
                  tt_ref, t_ref, f_ref, ft_ref, pad_buf, u_buf, s_buf, act_buf, du_buf,
                  g_sum, half_buf, mate_buf, far_buf, fin_buf,
-                 tg_ref, fg_ref, w_send, w_recv, w_loc, in_send, in_recv, o_send, o_recv, r_send, r_recv):
+                 tg_ref, fg_ref, w_send, w_recv, w_loc, in_send, in_recv, o_send, o_recv, r_send, r_recv, met, row_in):
     chunks, coefs = x_buf.shape[0], x_buf.shape[1]
     share = x_hbm.shape[1]
     own = chunks * LANES
@@ -59,9 +59,13 @@
     barrier = pltpu.get_barrier_semaphore()
     for flip in (1, 2, 3):
         pl.semaphore_signal(barrier, inc=1, device_id={'tp': me ^ flip}, device_id_type=MESH)
-    pl.semaphore_signal(barrier, inc=1, device_id={'dp': 1 - side}, device_id_type=MESH)
-    pl.semaphore_signal(barrier, inc=1, device_id={'dp': 1 - side, 'tp': mate}, device_id_type=MESH)
-    pl.semaphore_wait(barrier, 5)
+    hub = gain_in.shape[0] - 1
+
+    @pl.when(me == hub)
+    def _():
+        pl.semaphore_signal(barrier, inc=1, device_id={'dp': 1 - side}, device_id_type=MESH)
+
+    pl.semaphore_wait(barrier, 3 + (me == hub).astype(jnp.int32))
 
     def weight_parts(who):
         hid = up_hbm.shape[1]
@@ -153,6 +157,17 @@
     pad_buf[1:coefs, :points] = fg_ref[...].astype(BF16).astype(F32)
     ft_ref[...] = pad_buf[:STEP, :pts].astype(BF16)
     f_ref[...] = (0.5 * pad_buf[...]).T[:pts, :STEP].astype(BF16)
+
+    @pl.when(me == hub)
+    def _():
+        pl.semaphore_signal(met, inc=1, device_id={'dp': 1 - side}, device_id_type=MESH)
+        pl.semaphore_wait(met, 1)
+        for flip in (1, 2, 3):
+            pl.semaphore_signal(row_in, inc=1, device_id={'tp': me ^ flip}, device_id_type=MESH)
+
+    @pl.when(me != hub)
+    def _():
+        pl.semaphore_wait(row_in, 1)
 
     for copy in far_weights:
         copy.wait_recv()
@@ -426,7 +441,7 @@
                 pltpu.VMEM(to_grid.shape, F32), pltpu.VMEM(from_grid.shape[::-1], F32),
                 dma((3, 4)), dma((3, 4)), dma((2, 4)),
                 dma((2,)), dma((2, chunks)), dma((2,)), dma((2,)),
-                dma((4,)), dma((4,))],
+                dma((4,)), dma((4,)), pltpu.SemaphoreType.REGULAR, pltpu.SemaphoreType.REGULAR],
             compiler_params=pltpu.CompilerParams(collective_id=0, has_side_effects=True, vmem_limit_bytes=48 * 1024 * 1024),
             name='fused',
         )(x_t, g_t, up_t, gate_t, down_loc, gain_loc, to_grid, jnp.transpose(from_grid, (1, 0)))

time: 294 us -> 293 us (level)
  no operation moved by 1% of the time
where the time goes in v5:
time: 293 us
  Pallas kernels  292 us (100%)
    pallas_call x1, Pallas kernels, local_step(): pl.pallas_call(fused_kernel, out_shape=(pltpu.VMEM(x_t.shape, BF16), pltp...  288 us

profile of v5, /device:TPU:0, one launch (start us, length us, event | category | flops | bytes accessed | tf_op | source)
XLA Modules:
  0.0 292.9 jit_solution(4718777526177249160)
XLA Ops:
  0.6 287.6 %fused.1 = (bf16[49,32,2048]{2,1,0:T(8,128)(2,1)S(1)}, bf16[49,32,2048]{2,1,0:T(8,128)(2,1)S(1)}, bf16[15,64,128]{2,1,0:T(8,128)(2,1)S(1)}) custom-call(bf16[49,32,2048]{2,1,0:T(8,128)(2,1)} %bitcast.9, bf16[49,32,2048]{2,1,0:T(8,128)(2,1)} %bitcast.10, bf16[7,64,128]{2,1,0:T(8,128)(2,1)} %bitcast.11, bf16[64,128]{1,0:T(8,128)(2,1)} %bitcast.13, ...), custom_call_target="tpu_custom_call" | custom-call | tf_op jit(solution)/shard_map/fused/pallas_call | solution.py:423
  288.2 4.7 %write.1 = (bf16[49,32,2048]{2,1,0:T(8,128)(2,1)}, bf16[49,32,2048]{2,1,0:T(8,128)(2,1)}, bf16[7,64,128]{2,1,0:T(8,128)(2,1)}, bf16[64,128]{1,0:T(8,128)(2,1)}, bf16[7,64,128]{2,1,0:T(8,128)(2,1)}) custom-call(bf16[49,32,2048]{2,1,0:T(8,128)(2,1)S(1)} %get-tuple-element.13.out_vm, bf16[49,32,2048]{2,1,0:T(8,128)(2,1)S(1)} %get-tuple-element.14.dx_vm, ...), custom_call_target="tpu_custom_call" | custom-call | tf_op jit(solution)/shard_map/write/pallas_call | solution.py:448

commit v6 on v5

--- a/solution.py
+++ b/solution.py
@@ -59,7 +59,7 @@
     barrier = pltpu.get_barrier_semaphore()
     for flip in (1, 2, 3):
         pl.semaphore_signal(barrier, inc=1, device_id={'tp': me ^ flip}, device_id_type=MESH)
-    hub = gain_in.shape[0] - 1
+    hub = gain_in.shape[0] - 2
 
     @pl.when(me == hub)
     def _():
@@ -74,19 +74,23 @@
     sources = (up_hbm, down_hbm, gate_hbm, gain_hbm)
 
     def weight_copies(srcs, dsts, come, to, peer):
-        return [pltpu.make_async_remote_copy(src, dst, w_send.at[to, i], w_recv.at[come, i], device_id=peer, device_id_type=MESH)
+        return [pltpu.make_async_remote_copy(src, dst, w_send.at[to, i // 3], w_recv.at[come, i // 3], device_id=peer, device_id_type=MESH)
                 for i, (src, dst) in enumerate(zip(srcs, dsts))]
 
     crosses = lax.rem(me, 2) == side
     mine, far = weight_parts(me), weight_parts(me ^ 2)
-    own_weights = [pltpu.make_async_copy(src, dst, w_loc.at[0, i]) for i, (src, dst) in enumerate(zip(sources, mine))]
-    far_weights = weight_copies(sources, mine, 0, 0, {'tp': me ^ 2})
-    mate_weights = weight_copies(sources, mine, 1, 1, {'tp': mate})
-    passed_weights = (weight_copies(far, far, 2, 2, {'tp': mate}) + weight_copies(far, far, 0, 2, {'dp': 1 - side})
-                      + weight_copies(far, far, 2, 2, {'dp': 1 - side, 'tp': mate}))
+    own_weights = [pltpu.make_async_copy(src, dst, w_recv.at[1, i // 3]) for i, (src, dst) in enumerate(zip(sources, mine))]
+    far_weights = weight_copies(sources, mine, 0, 1, {'tp': me ^ 2})
+    mate_weights = weight_copies(sources, mine, 1, 0, {'tp': mate})
+    passed_weights = (weight_copies(far, far, 1, 1, {'tp': mate}) + weight_copies(far, far, 0, 1, {'dp': 1 - side})
+                      + weight_copies(far, far, 1, 1, {'dp': 1 - side, 'tp': mate}))
     hid = up_hbm.shape[1]
-    thrice = (wu.at[:, pl.ds(0, 3 * hid), :], wd.at[:, pl.ds(0, 3 * hid), :], wg.at[pl.ds(0, 3 * hid), :], gain_in.at[pl.ds(0, 3)])
-    grids = [pltpu.make_async_copy(tg_hbm, tg_ref, w_loc.at[1, 0]), pltpu.make_async_copy(fg_hbm, fg_ref, w_loc.at[1, 1])]
+    grids = [pltpu.make_async_copy(tg_hbm, tg_ref, w_loc.at[0]), pltpu.make_async_copy(fg_hbm, fg_ref, w_loc.at[1])]
+
+    def drain_slices(count, sem):
+        drain(n_buf.at[pl.ds(0, count * fin_buf.shape[0] // 2 if count % 2 == 0 else count * fin_buf.shape[0]),
+                       pl.ds(0, LANES if count % 2 == 0 else hid), :], sem.at[0])
+        drain(gain_in.at[pl.ds(0, count)], sem.at[1])
 
     @pl.when(crosses)
     def _():
@@ -100,12 +104,12 @@
         src, buf = ((x_hbm, x_buf), (g_hbm, g_buf))[tensor]
         return pltpu.make_async_remote_copy(
             src.at[:, :, lanes(me ^ flip, chunk)], buf.at[chunk, :, rows(me, share), :],
-            in_send.at[tensor], in_recv.at[tensor, chunk],
+            in_send.at[tensor], in_recv.at[chunk],
             device_id={'tp': me ^ flip}, device_id_type=MESH)
 
     def input_local(tensor, chunk):
         src, buf = ((x_hbm, x_buf), (g_hbm, g_buf))[tensor]
-        return pltpu.make_async_copy(src.at[:, :, lanes(me, chunk)], buf.at[chunk, :, rows(me, share), :], in_recv.at[tensor, chunk])
+        return pltpu.make_async_copy(src.at[:, :, lanes(me, chunk)], buf.at[chunk, :, rows(me, share), :], in_recv.at[chunk])
 
     def output_copy(tensor, chunk, flip):
         buf, dst = ((o_buf, out_vm), (g_buf, dx_vm))[tensor]
@@ -169,21 +173,16 @@
     def _():
         pl.semaphore_wait(row_in, 1)
 
-    for copy in far_weights:
-        copy.wait_recv()
+    drain_slices(1, w_recv.at[0])
 
     @pl.when(crosses)
     def _():
         for copy in passed_weights:
             copy.start()
-        for i, copy in enumerate(far_weights):
-            copy.wait_send()
-            drain(thrice[i], w_send.at[2, i])
-
-    for copy in passed_weights[:len(sources)]:
-        copy.wait_recv()
-    for copy in mate_weights + own_weights:
-        copy.wait()
+        drain_slices(4, w_send.at[1])
+
+    drain_slices(3, w_recv.at[1])
+    drain_slices(1, w_send.at[0])
 
     def turn(deg, carry):
         wut[deg] = wu[deg].astype(F32).T.astype(BF16)
@@ -203,8 +202,7 @@
     inv_vec = 1.0 / (LANES * (coefs - 1))
 
     def chunk_step(chunk, carry):
-        for tensor, buf in enumerate((x_buf, g_buf)):
-            drain(buf.at[chunk], in_recv.at[tensor, chunk])
+        drain(x_buf.at[pl.ds(0, 2)], in_recv.at[chunk])
 
         def square_sum(k, acc):
             val = x_buf[chunk, k].astype(F32)
@@ -329,7 +327,7 @@
         return pl.ds(pl.multiple_of(who * hid + where * part, part), part)
 
     def push(src, dst, num, peer):
-        return pltpu.make_async_remote_copy(src, dst, r_send.at[num], r_recv.at[num], device_id=peer, device_id_type=MESH)
+        return pltpu.make_async_remote_copy(src, dst, r_send, r_recv.at[num], device_id=peer, device_id_type=MESH)
 
     for n in range(slices):
         push(g_sum.at[:, sum_rows(n, 1 - side), :], half_buf.at[n], 0, {'dp': 1 - side}).start()
@@ -345,7 +343,6 @@
     push(half_buf.at[mate], mate_buf.at[0], 1, {'tp': mate}).start()
     push(half_buf.at[mate ^ 2], mate_buf.at[1], 1, {'tp': mate}).start()
     drain(mate_buf, r_recv.at[1])
-    drain(mate_buf, r_send.at[1])
 
     def add_mate(row, carry):
         mate_buf[0, row] += half_buf[me, row]
@@ -358,7 +355,7 @@
     for tensor in (0, 1):
         for flip in (2, 3):
             output_copy(tensor, chunks - 1, flip).start()
-    cross.wait()
+    cross.wait_recv()
     ours = pl.ds(pl.multiple_of(side * part, part), part)
 
     def add_far(row, carry):
@@ -368,8 +365,8 @@
     lax.fori_loop(0, rows_all, add_far, 0)
     last = push(fin_buf.at[:, ours, :], fin_buf.at[:, ours, :], 3, {'dp': 1 - side})
     last.start()
-    last.wait()
-    drain(half_buf, r_send.at[0])
+    last.wait_recv()
+    drain(g_sum.at[:, pl.ds(0, slices * hid * 15 // 16), :], r_send)
     fin_vm[...] = fin_buf[...]
 
     for tensor, (buf, dst) in enumerate(((o_buf, out_vm), (g_buf, dx_vm))):
@@ -380,19 +377,16 @@
 
 
 def write_kernel(out_vm, dx_vm, fin_vm, out_hbm, dx_hbm, dup_hbm, dgate_hbm, ddown_hbm, sems):
-    coefs, step = out_hbm.shape[0], 7
+    coefs, step = out_hbm.shape[0], 1
     degrees = dup_hbm.shape[0]
     for start in range(0, coefs, step):
         span = pl.ds(start, step)
         pltpu.make_async_copy(out_vm.at[span], out_hbm.at[span], sems.at[0]).start()
         pltpu.make_async_copy(dx_vm.at[span], dx_hbm.at[span], sems.at[1]).start()
-    small = [pltpu.make_async_copy(fin_vm.at[pl.ds(0, degrees)], dup_hbm, sems.at[2]),
-             pltpu.make_async_copy(fin_vm.at[pl.ds(degrees, degrees)], ddown_hbm, sems.at[3]),
-             pltpu.make_async_copy(fin_vm.at[2 * degrees], dgate_hbm, sems.at[4])]
-    for copy in small:
-        copy.start()
-    for copy in small:
-        copy.wait()
+    pltpu.make_async_copy(fin_vm.at[pl.ds(0, degrees)], dup_hbm, sems.at[2]).start()
+    pltpu.make_async_copy(fin_vm.at[pl.ds(degrees, degrees)], ddown_hbm, sems.at[2]).start()
+    pltpu.make_async_copy(fin_vm.at[2 * degrees], dgate_hbm, sems.at[2]).start()
+    pltpu.make_async_copy(fin_vm, fin_vm, sems.at[2]).wait()
     pltpu.make_async_copy(out_vm, out_hbm, sems.at[0]).wait()
     pltpu.make_async_copy(dx_vm, dx_hbm, sems.at[1]).wait()
 
@@ -439,9 +433,9 @@
                 pltpu.VMEM((2, 2 * degrees + 1, hid // 2, channels), F32), pltpu.VMEM((2 * degrees + 1, hid // 2, channels), F32),
                 pltpu.VMEM((2 * degrees + 1, hid, channels), BF16),
                 pltpu.VMEM(to_grid.shape, F32), pltpu.VMEM(from_grid.shape[::-1], F32),
-                dma((3, 4)), dma((3, 4)), dma((2, 4)),
-                dma((2,)), dma((2, chunks)), dma((2,)), dma((2,)),
-                dma((4,)), dma((4,)), pltpu.SemaphoreType.REGULAR, pltpu.SemaphoreType.REGULAR],
+                dma((2, 2)), dma((2, 2)), dma((2,)),
+                dma((2,)), dma((chunks,)), dma((2,)), dma((2,)),
+                dma(()), dma((4,)), pltpu.SemaphoreType.REGULAR, pltpu.SemaphoreType.REGULAR],
             compiler_params=pltpu.CompilerParams(collective_id=0, has_side_effects=True, vmem_limit_bytes=48 * 1024 * 1024),
             name='fused',
         )(x_t, g_t, up_t, gate_t, down_loc, gain_loc, to_grid, jnp.transpose(from_grid, (1, 0)))
@@ -455,7 +449,7 @@
                 jax.ShapeDtypeStruct((degrees, hid, channels), BF16)),
             in_specs=[vmem] * 3,
             out_specs=(hbm,) * 5,
-            scratch_shapes=[dma((5,))],
+            scratch_shapes=[dma((3,))],
             compiler_params=pltpu.CompilerParams(vmem_limit_bytes=1024 * 1024),
             name='write',
         )(out_v, dx_v, fin_v)

time: 293 us -> 293 us (level)
  no operation moved by 1% of the time
where the time goes in v6:
time: 293 us
  Pallas kernels  292 us (100%)
    pallas_call x1, Pallas kernels, local_step(): pl.pallas_call(fused_kernel, out_shape=(pltpu.VMEM(x_t.shape, BF16), pltp...  287 us

profile of v6, /device:TPU:0, one launch (start us, length us, event | category | flops | bytes accessed | tf_op | source)
XLA Modules:
  0.0 292.6 jit_solution(4727044671978853635)
XLA Ops:
  0.6 287.3 %fused.1 = (bf16[49,32,2048]{2,1,0:T(8,128)(2,1)S(1)}, bf16[49,32,2048]{2,1,0:T(8,128)(2,1)S(1)}, bf16[15,64,128]{2,1,0:T(8,128)(2,1)S(1)}) custom-call(bf16[49,32,2048]{2,1,0:T(8,128)(2,1)} %bitcast.9, bf16[49,32,2048]{2,1,0:T(8,128)(2,1)} %bitcast.10, bf16[7,64,128]{2,1,0:T(8,128)(2,1)} %bitcast.11, bf16[64,128]{1,0:T(8,128)(2,1)} %bitcast.13, ...), custom_call_target="tpu_custom_call" | custom-call | tf_op jit(solution)/shard_map/fused/pallas_call | solution.py:417
  288.0 4.6 %write.1 = (bf16[49,32,2048]{2,1,0:T(8,128)(2,1)}, bf16[49,32,2048]{2,1,0:T(8,128)(2,1)}, bf16[7,64,128]{2,1,0:T(8,128)(2,1)}, bf16[64,128]{1,0:T(8,128)(2,1)}, bf16[7,64,128]{2,1,0:T(8,128)(2,1)}) custom-call(bf16[49,32,2048]{2,1,0:T(8,128)(2,1)S(1)} %get-tuple-element.13.out_vm, bf16[49,32,2048]{2,1,0:T(8,128)(2,1)S(1)} %get-tuple-element.14.dx_vm, ...), custom_call_target="tpu_custom_call" | custom-call | tf_op jit(solution)/shard_map/write/pallas_call | solution.py:442

commit v7 on v6

--- a/solution.py
+++ b/solution.py
@@ -77,7 +77,7 @@
         return [pltpu.make_async_remote_copy(src, dst, w_send.at[to, i // 3], w_recv.at[come, i // 3], device_id=peer, device_id_type=MESH)
                 for i, (src, dst) in enumerate(zip(srcs, dsts))]
 
-    crosses = lax.rem(me, 2) == side
+    crosses = lax.rem(me, 2) != side
     mine, far = weight_parts(me), weight_parts(me ^ 2)
     own_weights = [pltpu.make_async_copy(src, dst, w_recv.at[1, i // 3]) for i, (src, dst) in enumerate(zip(sources, mine))]
     far_weights = weight_copies(sources, mine, 0, 1, {'tp': me ^ 2})
@@ -353,7 +353,7 @@
     cross = push(mate_buf.at[1], far_buf, 2, {'tp': me ^ 2})
     cross.start()
     for tensor in (0, 1):
-        for flip in (2, 3):
+        for flip in (3, 2):
             output_copy(tensor, chunks - 1, flip).start()
     cross.wait_recv()
     ours = pl.ds(pl.multiple_of(side * part, part), part)

time: 293 us -> 293 us (level)
  no operation moved by 1% of the time
where the time goes in v7:
time: 293 us
  Pallas kernels  292 us (100%)
    pallas_call x1, Pallas kernels, local_step(): pl.pallas_call(fused_kernel, out_shape=(pltpu.VMEM(x_t.shape, BF16), pltp...  287 us

profile of v7, /device:TPU:0, one launch (start us, length us, event | category | flops | bytes accessed | tf_op | source)
XLA Modules:
  0.0 292.5 jit_solution(4950089499236117841)
XLA Ops:
  0.6 287.2 %fused.1 = (bf16[49,32,2048]{2,1,0:T(8,128)(2,1)S(1)}, bf16[49,32,2048]{2,1,0:T(8,128)(2,1)S(1)}, bf16[15,64,128]{2,1,0:T(8,128)(2,1)S(1)}) custom-call(bf16[49,32,2048]{2,1,0:T(8,128)(2,1)} %bitcast.9, bf16[49,32,2048]{2,1,0:T(8,128)(2,1)} %bitcast.10, bf16[7,64,128]{2,1,0:T(8,128)(2,1)} %bitcast.11, bf16[64,128]{1,0:T(8,128)(2,1)} %bitcast.13, ...), custom_call_target="tpu_custom_call" | custom-call | tf_op jit(solution)/shard_map/fused/pallas_call | solution.py:417
  287.9 4.6 %write.1 = (bf16[49,32,2048]{2,1,0:T(8,128)(2,1)}, bf16[49,32,2048]{2,1,0:T(8,128)(2,1)}, bf16[7,64,128]{2,1,0:T(8,128)(2,1)}, bf16[64,128]{1,0:T(8,128)(2,1)}, bf16[7,64,128]{2,1,0:T(8,128)(2,1)}) custom-call(bf16[49,32,2048]{2,1,0:T(8,128)(2,1)S(1)} %get-tuple-element.13.out_vm, bf16[49,32,2048]{2,1,0:T(8,128)(2,1)S(1)} %get-tuple-element.14.dx_vm, ...), custom_call_target="tpu_custom_call" | custom-call | tf_op jit(solution)/shard_map/write/pallas_call | solution.py:442
